TPU v7x, 512 devices: a 4x2x32 block of a 4x8x32 slice. The times are simulated.
512 devices in a mesh: members: 2 (over y), elem: 64 (over z, core), lev: 4 (over x).
Axes of the slice: x: 4, y: 2, z: 32, core: 2. Of those that a mesh axis runs over, the one named last changes fastest.
The devices are a block of a 4x8x32 slice.
Arguments:
- tracers: float32 [25, 8, 16, 32768], P(None, 'lev', None, ('members', 'elem')), parts along dimension 3, may hold values from -6 to 6
- layer_mass: float32 [8, 16, 32768], P('lev', None, ('members', 'elem')), parts along dimension 2, may hold values from 0.3 to 2.7
- winds: float32 [2, 8, 16, 32768], P(None, 'lev', None, ('members', 'elem')), parts along dimension 3, may hold values from 0.5 to 1.5
- metric: float32 [16, 16384], P(None, 'elem'), may hold values from 0.6 to 1.6
- neighbours: int32 [16384, 8], P('elem'), may hold values from 0 to 16383, as said below
Outputs:
- tracers_out: float32 [25, 8, 16, 32768], P(None, 'lev', None, ('members', 'elem')), parts along dimension 3
- surface: float32 [16, 32768], P(None, ('members', 'elem')), parts along dimension 1
There are 2 independent parts, one for each index of `members`. A program takes and returns all parts, laid end to end along the dimension named above; an argument that names none is the same for every part. Nothing has to cross between parts.
Inputs may be any that keep to these rules, and one draw needn't show every extreme that they name: `neighbours`: the grid has 128 columns and 128 rows of elements; it is periodic north to south, and east of column 127 of row y lies column 0 of row y + 16 (rows modulo 128). Block b of 256 elements along elem is the square patch of 16 by 16 elements in patch row b // 8 and patch column b % 8, its elements in a drawn order; so the east, west, north and south patches of block b are blocks b + 1, b - 1, b + 8, b - 8 and the diagonal ones b + 9, b + 7, b - 7, b - 8 - 1 (all modulo the number of blocks). Adjacency is symmetric.
All inputs are finite; a program needn't handle non-finite values.
Results may differ from a plain program's by a relative error of at most 0.0003.
Values sent between devices are 32-bit elements; how exact they have to be, the bound alone decides.
A program may use at most 128 MiB of HBM per device.

v0:
```python
import math

import jax
import jax.numpy as jnp
import numpy as np
from jax import lax
from jax.sharding import PartitionSpec as P

PSIDE = 16


time_step = 0.035


def shifted(block, axis, distance):
    devices = range(lax.axis_size(axis))
    route = [((i - distance) % len(devices), i) for i in devices]
    return lax.ppermute(block, axis, route)


def copy_for_each(array, axis):
    copies = jnp.broadcast_to(array, (lax.axis_size(axis), *array.shape))
    return lax.all_to_all(copies, axis, split_axis=0, concat_axis=0, tiled=True)


def joined_along(pieces, dim):
    dims = list(pieces.shape[1:])
    dims[dim] *= pieces.shape[0]
    return jnp.moveaxis(pieces, 0, dim).reshape(dims)


def collect(array, axis, dim):
    pieces = copy_for_each(array, axis)
    return joined_along(pieces, dim)


def extended_2(cells, sides, width):
    for axis, dim in sides:
        count = lax.axis_size(axis)
        ends = count - 1
        head = lax.slice_in_dim(cells, 0, width, axis=dim)
        tail = lax.slice_in_dim(cells, cells.shape[dim] - width, cells.shape[dim], axis=dim)
        cells = jnp.concatenate(
            [
                lax.ppermute(tail, axis, [(i, (i + 1) % count) for i in range(ends)]),
                cells,
                lax.ppermute(head, axis, [((i + 1) % count, i) for i in range(ends)]),
            ],
            axis=dim,
        )
    return cells


def lagrange_scale(points, which):
    product = 1.0
    for other in range(4):
        if other != which:
            product = product * (points[which] - points[other])
    return product


def node_tables():
    points = np.array([-1.0, -1.0 / math.sqrt(5.0), 1.0 / math.sqrt(5.0), 1.0])
    weights = np.array([1.0, 5.0, 5.0, 1.0]) / 6.0
    derivative = np.zeros((4, 4))
    for target in range(4):
        for source in range(4):
            if target == source:
                derivative[target, source] = sum(
                    (
                        1.0 / (points[target] - points[other])
                        for other in range(4)
                        if other != target
                    )
                )
            else:
                derivative[target, source] = lagrange_scale(points, target) / (
                    lagrange_scale(points, source) * (points[target] - points[source])
                )
    return (
        np.kron(np.eye(4), derivative),
        np.kron(derivative, np.eye(4)),
        np.kron(weights, weights),
    )


def side_links():
    column = list(range(4))
    return [
        ([4 * step + 3 for step in column], [4 * step for step in column]),
        ([4 * step for step in column], [4 * step + 3 for step in column]),
        ([12 + step for step in column], [step for step in column]),
        ([step for step in column], [12 + step for step in column]),
        ([15], [0]),
        ([12], [3]),
        ([3], [12]),
        ([0], [15]),
    ]


def link_table():
    table = np.zeros((8, 16, 16), np.float32)
    for direction, pair in enumerate(side_links()):
        for target, source in zip(pair[0], pair[1]):
            table[direction, source, target] = 1.0
    return table


def apply_table(table, field):
    return jnp.einsum(
        "nm,...me->...ne", jnp.asarray(table, jnp.float32), field, precision=lax.Precision.HIGHEST
    )


def tendency(state, winds, metric):
    along_east, along_north, weights = node_tables()
    east_flux = metric * winds[0] * state
    north_flux = metric * winds[1] * state
    return -(apply_table(along_east, east_flux) + apply_table(along_north, north_flux)) / metric


def assemble_rows(rows, extended, positions):
    flat_index = jnp.transpose(positions).reshape(-1)
    picked = jnp.take(extended, flat_index, axis=0).reshape((8,) + rows.shape)
    placed = jnp.einsum(
        "dwfm,dmn->wfn", picked, jnp.asarray(link_table()), precision=lax.Precision.HIGHEST
    )
    return rows + placed


def pack_order(flags, slots):
    ranks = jnp.cumsum(flags.astype(jnp.int32)) - 1
    match = flags[:, None] & (ranks[:, None] == jnp.arange(slots, dtype=jnp.int32)[None, :])
    return jnp.sum(
        jnp.where(match, jnp.arange(flags.shape[0], dtype=jnp.int32)[:, None], 0), axis=0
    )


def referenced(within, chosen, width):
    found = (within[:, :, None] == jnp.arange(width, dtype=jnp.int32)[None, None, :]) & chosen[
        :, :, None
    ]
    return jnp.any(found, axis=(0, 1)).astype(jnp.int32)


def per_device(tracers, layer_mass, winds, metric, neighbours):
    width = metric.shape[-1]
    count = lax.axis_size("elem")
    place = lax.axis_index("elem")
    across = min(8, max(2, count // 8))
    weights = node_tables()[2]
    mass = jnp.asarray(weights, jnp.float32)[:, None] * metric
    owner = neighbours // width
    within = neighbours % width
    relation = (owner - place) % count
    roles = [
        (1, PSIDE),
        (-1, PSIDE),
        (across, PSIDE),
        (-across, PSIDE),
        (across + 1, 1),
        (across - 1, 1),
        (1 - across, 1),
        (-1 - across, 1),
    ]
    slot_sizes = {}
    for offset, amount in roles:
        key_rel = offset % count
        slot_sizes[key_rel] = slot_sizes.get(key_rel, 0) + amount
    peers = sorted(slot_sizes.keys())
    orders = []
    positions = within
    start = width
    for peer in peers:
        slots = min(slot_sizes[peer], width)
        orders.append(
            (peer, pack_order(jnp.any(relation == (count - peer) % count, axis=1), slots))
        )
        rank = jnp.cumsum(referenced(within, relation == peer, width)) - 1
        positions = jnp.where(relation == peer, start + rank[within], positions)
        start = start + slots

    def extend(rows):
        pieces = [rows]
        for peer, order in orders:
            packed = jnp.take(rows, order, axis=0)
            pieces.append(shifted(packed, "elem", -peer))
        return jnp.concatenate(pieces, axis=0)

    start_state = jnp.concatenate([layer_mass[None], tracers * layer_mass[None]], axis=0)
    first_rate = tendency(start_state, winds, metric)
    first_flat = jnp.concatenate(
        [mass[None], (mass * first_rate).reshape((-1,) + first_rate.shape[2:])], axis=0
    )
    first_rows = jnp.transpose(first_flat, (2, 0, 1))
    first_sum = jnp.transpose(assemble_rows(first_rows, extend(first_rows), positions), (1, 2, 0))
    shared = first_sum[0]
    middle_state = start_state + time_step * (first_sum[1:] / shared).reshape(first_rate.shape)
    second_rate = tendency(middle_state, winds, metric)
    second_flat = (mass * second_rate).reshape((-1,) + second_rate.shape[2:])
    second_rows = jnp.transpose(second_flat, (2, 0, 1))
    second_sum = jnp.transpose(
        assemble_rows(second_rows, extend(second_rows), positions), (1, 2, 0)
    )
    final_state = 0.5 * (
        start_state + middle_state + time_step * (second_sum / shared).reshape(second_rate.shape)
    )
    thick = final_state[0]
    carried = final_state[1:]
    levels_here = thick.shape[0]
    total_levels = levels_here * lax.axis_size("lev")
    column = jnp.sum(thick, axis=0)
    every = collect(column[None], "lev", 0)
    surface = jnp.sum(every, axis=0)
    lower_blocks = jnp.arange(lax.axis_size("lev"), dtype=jnp.int32)[
        :, None, None
    ] < lax.axis_index("lev")
    below_sum = jnp.sum(jnp.where(lower_blocks, every, 0.0), axis=0)
    edges = (
        lax.axis_index("lev") * levels_here + jnp.arange(levels_here + 1, dtype=jnp.int32)
    ).astype(jnp.float32)
    fraction = (edges + edges * (edges - 1.0) / (total_levels - 1)) / (2.0 * total_levels)
    layers = edges[:-1]
    share = (1.0 + 2.0 * layers / (total_levels - 1)) / (2.0 * total_levels)
    above_mass = below_sum[None] + jnp.concatenate(
        [jnp.zeros_like(column)[None], jnp.cumsum(thick, axis=0)], axis=0
    )
    delta = above_mass - surface * fraction[:, None, None]
    ratio = carried / thick
    padded = extended_2(ratio, (("lev", 1),), 1)
    flux = delta * jnp.where(delta > 0.0, padded[:, :-1], padded[:, 1:])
    result = (carried + flux[:, :-1] - flux[:, 1:]) / (surface * share[:, None, None])
    return (result, surface)


def solution(mesh):
    placed = (
        P(None, "lev", None, ("members", "elem")),
        P("lev", None, ("members", "elem")),
        P(None, "lev", None, ("members", "elem")),
        P(None, "elem"),
        P("elem", None),
    )
    return jax.shard_map(
        per_device,
        mesh=mesh,
        in_specs=placed,
        out_specs=(P(None, "lev", None, ("members", "elem")), P(None, ("members", "elem"))),
        check_vma=False,
    )
```

profile of v0, /device:TPU:33, one launch (start us, length us, event | category | flops | bytes accessed | tf_op | source)
XLA Modules:
  0.0 539.6 jit_solution(13766275498095320236)
XLA Ops:
  20.8 1.7 dynamic-slice_select_fusion
  22.5 45.5 %collective-permute-start.1 = (f32[1,53,16]{0,2,1:T(8,128)}, f32[1,53,16]{0,2,1:T(8,128)}, u32[]{:S(2)}, u32[]{:S(2)}) collective-permute-start(f32[1,53,16]{0,2,1:T(8,128)} %get-tuple-element.62), channel_id=1, source_target_pairs={{28,0},{32,4},{36,8},{40,12},{44,16},{48,20},{52,24},{56,28},{60,3... | collective-permute-start | bytes 10184 | tf_op jit(solution)/shard_map/ppermute | solution.py:18
  68.0 2.0 collective-permute-start.3
  70.0 8.5 %collective-permute-start.4 = (f32[1,53,16]{0,2,1:T(8,128)}, f32[1,53,16]{0,2,1:T(8,128)}, u32[]{:S(2)}, u32[]{:S(2)}) collective-permute-start(f32[1,53,16]{0,2,1:T(8,128)} %get-tuple-element.60), channel_id=1, source_target_pairs={{220,0},{224,4},{228,8},{232,12},{236,16},{240,20},{244,24},{248,2... | collective-permute-start | bytes 10184 | tf_op jit(solution)/shard_map/ppermute | solution.py:18
  78.5 2.0 collective-permute-start.6
  80.4 1.5 copy.110
  85.6 4.3 collective-permute-start.5
  93.8 3.7 fusion.23
  98.8 13.1 %gather_fusion = s32[2048]{0:T(1024)S(1)} fusion(s32[256]{0:T(256)S(1)} %add_bitcast_fusion.11, s32[2048]{0:T(1024)S(1)} %broadcast_clamp_fusion.1), kind=kCustom, calls=%fused_computation.8 | custom fusion | bytes 24576 | tf_op jit(solution)/shard_map/gather | solution.py:180
  112.8 13.1 %gather_fusion.1 = s32[2048]{0:T(1024)S(1)} fusion(s32[256]{0:T(256)S(1)} %add_bitcast_fusion.10, s32[2048]{0:T(1024)S(1)} %broadcast_clamp_fusion.1), kind=kCustom, calls=%fused_computation.9 | custom fusion | bytes 24576 | tf_op jit(solution)/shard_map/gather | solution.py:180
  127.8 13.1 %gather_fusion.2 = s32[2048]{0:T(1024)S(1)} fusion(s32[256]{0:T(256)S(1)} %add_bitcast_fusion.9, s32[2048]{0:T(1024)S(1)} %broadcast_clamp_fusion.1), kind=kCustom, calls=%fused_computation.10 | custom fusion | bytes 24576 | tf_op jit(solution)/shard_map/gather | solution.py:180
  141.7 13.1 %gather_fusion.3 = s32[2048]{0:T(1024)S(1)} fusion(s32[256]{0:T(256)S(1)} %add_bitcast_fusion.8, s32[2048]{0:T(1024)S(1)} %broadcast_clamp_fusion.1), kind=kCustom, calls=%fused_computation.11 | custom fusion | bytes 24576 | tf_op jit(solution)/shard_map/gather | solution.py:180
  156.7 13.1 %gather_fusion.4 = s32[2048]{0:T(1024)S(1)} fusion(s32[256]{0:T(256)S(1)} %add_bitcast_fusion.7, s32[2048]{0:T(1024)S(1)} %broadcast_clamp_fusion.1), kind=kCustom, calls=%fused_computation.12 | custom fusion | bytes 24576 | tf_op jit(solution)/shard_map/gather | solution.py:180
  170.1 13.1 %gather_fusion.5 = s32[2048]{0:T(1024)S(1)} fusion(s32[256]{0:T(256)S(1)} %add_bitcast_fusion.6, s32[2048]{0:T(1024)S(1)} %broadcast_clamp_fusion.1), kind=kCustom, calls=%fused_computation.13 | custom fusion | bytes 24576 | tf_op jit(solution)/shard_map/gather | solution.py:180
  184.4 13.1 %gather_fusion.6 = s32[2048]{0:T(1024)S(1)} fusion(s32[256]{0:T(256)S(1)} %add_bitcast_fusion.5, s32[2048]{0:T(1024)S(1)} %broadcast_clamp_fusion.1), kind=kCustom, calls=%fused_computation.14 | custom fusion | bytes 24576 | tf_op jit(solution)/shard_map/gather | solution.py:180
  197.8 13.1 %gather_fusion.7 = s32[2048]{0:T(1024)S(1)} fusion(s32[256]{0:T(256)S(1)} %add_bitcast_fusion.4, s32[2048]{0:T(1024)S(1)} %broadcast_clamp_fusion.1), kind=kCustom, calls=%fused_computation.15 | custom fusion | bytes 24576 | tf_op jit(solution)/shard_map/gather | solution.py:180
  211.2 1.6 compare_and_fusion
  218.1 5.3 collective-permute-start.2
  224.4 2.4 collective-permute-start
  228.1 33.6 %collective-permute-done.2 = f32[16,53,16]{0,2,1:T(8,128)S(1)} collective-permute-done((f32[16,53,16]{0,2,1:T(8,128)S(1)}, f32[16,53,16]{0,2,1:T(8,128)S(1)}, u32[]{:S(2)}, u32[]{:S(2)}) %collective-permute-start.2) | collective-permute-done | bytes 54304 | tf_op jit(solution)/shard_map/ppermute | solution.py:18
  261.6 6.1 %collective-permute-done = f32[16,53,16]{0,2,1:T(8,128)S(1)} collective-permute-done((f32[16,53,16]{0,2,1:T(8,128)S(1)}, f32[16,53,16]{0,2,1:T(8,128)S(1)}, u32[]{:S(2)}, u32[]{:S(2)}) %collective-permute-start) | collective-permute-done | bytes 54304 | tf_op jit(solution)/shard_map/ppermute | solution.py:18
  267.8 4.3 concatenate.24
  272.0 2.4 copy.119
  274.4 20.7 %gather_fusion.8 = f32[2048,53,16]{1,2,0:T(8,128)} fusion(f32[324,53,16]{1,2,0:T(8,128)S(1)} %copy.119, s32[2048]{0:T(1024)S(1)} %broadcast_clamp_fusion), kind=kCustom, calls=%fused_computation.16 | custom fusion | bytes 13901824 | tf_op jit(solution)/shard_map/jit(_take)/gather | solution.py:124
  295.1 14.9 %copy.120 = f32[8,256,53,16]{1,3,0,2:T(8,128)} copy(f32[8,256,53,16]{2,3,1,0:T(8,128)} %bitcast.174) | data formatting | bytes 13893632 | tf_op jit(solution)/shard_map/jit(_take)/gather | solution.py:124
  310.1 6.1 %fusion.38 = f32[53,16,256]{2,1,0:T(8,128)S(1)} fusion(f32[8,16,16,1]{1,2,0,3:T(8,128)S(1)} %copy-done.33, f32[8,256,53,16]{1,3,0,2:T(8,128)} %copy.120, pred[8,256]{1,0:T(8,128)(4,1)S(1)} %copy.109, f32[52,16,256]{2,1,0:T(8,128)S(1)} %bitcast.183, f32[1,16,256]{2,1,0:T(8,128)S(1)} %copy-done.36), kind=kOutput, calls=%fused_computation.55 | convolution fusion | flops 335618048 | bytes 8693760 | tf_op jit(solution)/shard_map/dwfm,dmn->wfn/dot_general | solution.py:125
  319.4 1.5 copy.122
  323.0 1.7 dynamic-slice_select_fusion.4
  325.8 2.0 collective-permute-start.13
  328.6 7.6 %collective-permute-start.11 = (f32[1,52,16]{0,2,1:T(8,128)}, f32[1,52,16]{0,2,1:T(8,128)S(1)}, u32[]{:S(2)}, u32[]{:S(2)}) collective-permute-start(f32[1,52,16]{0,2,1:T(8,128)} %get-tuple-element.67), channel_id=1, source_target_pairs={{36,0},{40,4},{44,8},{48,12},{52,16},{56,20},{60,24},{64,28},{68,3... | collective-permute-start | bytes 9992 | tf_op jit(solution)/shard_map/ppermute | solution.py:18
  336.2 2.8 collective-permute-start.12
  339.0 3.1 collective-permute-start.14
  343.1 34.5 %collective-permute-done.11 = f32[1,52,16]{0,2,1:T(8,128)S(1)} collective-permute-done((f32[1,52,16]{0,2,1:T(8,128)}, f32[1,52,16]{0,2,1:T(8,128)S(1)}, u32[]{:S(2)}, u32[]{:S(2)}) %collective-permute-start.11) | collective-permute-done | bytes 3360 | tf_op jit(solution)/shard_map/ppermute | solution.py:18
  377.6 7.8 %collective-permute-start.10 = (f32[16,52,16]{0,2,1:T(8,128)S(1)}, f32[16,52,16]{0,2,1:T(8,128)S(1)}, u32[]{:S(2)}, u32[]{:S(2)}) collective-permute-start(f32[16,52,16]{0,2,1:T(8,128)S(1)} %broadcast_select_fusion.6), channel_id=1, source_target_pairs={{32,0},{36,4},{40,8},{44,12},{48,16},{52,20},{56,24},{60,28},{64,3... | collective-permute-start | bytes 159752 | tf_op jit(solution)/shard_map/ppermute | solution.py:18
  385.4 35.8 %collective-permute-done.12 = f32[1,52,16]{0,2,1:T(8,128)} collective-permute-done((f32[1,52,16]{0,2,1:T(8,128)}, f32[1,52,16]{0,2,1:T(8,128)}, u32[]{:S(2)}, u32[]{:S(2)}) %collective-permute-start.12) | collective-permute-done | bytes 3360 | tf_op jit(solution)/shard_map/ppermute | solution.py:18
  421.1 14.6 %collective-permute-start.9 = (f32[1,52,16]{0,2,1:T(8,128)}, f32[1,52,16]{0,2,1:T(8,128)S(1)}, u32[]{:S(2)}, u32[]{:S(2)}) collective-permute-start(f32[1,52,16]{0,2,1:T(8,128)} %get-tuple-element.68), channel_id=1, source_target_pairs={{28,0},{32,4},{36,8},{40,12},{44,16},{48,20},{52,24},{56,28},{60,3... | collective-permute-start | bytes 9992 | tf_op jit(solution)/shard_map/ppermute | solution.py:18
  435.7 4.7 collective-permute-done.14
  441.1 23.0 %collective-permute-done.9 = f32[1,52,16]{0,2,1:T(8,128)S(1)} collective-permute-done((f32[1,52,16]{0,2,1:T(8,128)}, f32[1,52,16]{0,2,1:T(8,128)S(1)}, u32[]{:S(2)}, u32[]{:S(2)}) %collective-permute-start.9) | collective-permute-done | bytes 3360 | tf_op jit(solution)/shard_map/ppermute | solution.py:18
  464.9 3.3 collective-permute-done.8
  468.2 4.3 concatenate.25
  472.5 2.3 copy.130
  474.8 20.8 %gather_fusion.9 = f32[2048,52,16]{1,2,0:T(8,128)} fusion(f32[324,52,16]{1,2,0:T(8,128)S(1)} %copy.130, s32[2048]{0:T(1024)} %copy-done.38), kind=kCustom, calls=%fused_computation.17 | custom fusion | bytes 13639680 | tf_op jit(solution)/shard_map/jit(_take)/gather | solution.py:124
  495.7 14.8 %copy.131 = f32[8,256,52,16]{1,3,0,2:T(8,128)} copy(f32[8,256,52,16]{2,3,1,0:T(8,128)} %bitcast.173) | data formatting | bytes 13631488 | tf_op jit(solution)/shard_map/jit(_take)/gather | solution.py:124
  510.5 6.1 %fusion.48 = f32[52,16,256]{2,1,0:T(8,128)S(1)} fusion(f32[52,16,256]{2,1,0:T(8,128)S(1)} %bitcast.178, f32[8,16,16,1]{1,2,0,3:T(8,128)S(1)} %copy-done.34, f32[8,256,52,16]{1,3,0,2:T(8,128)} %copy.131, pred[8,256]{1,0:T(8,128)(4,1)S(1)} %copy-done.46, f32[16,256]{1,0:T(8,128)S(1)} %slice_bitcast_fusion.1), kind=kOutput, calls=%fused_computation.60 | convolution fusion | flops 329498624 | bytes 8546304 | tf_op jit(solution)/shard_map/dwfm,dmn->wfn/dot_general | solution.py:125
  517.6 4.5 all-to-all-start
  522.3 3.4 collective-permute-start.16
  527.4 6.7 %collective-permute-done.16 = f32[25,1,16,256]{3,2,1,0:T(8,128)S(1)} collective-permute-done((f32[25,1,16,256]{3,2,1,0:T(8,128)S(1)}, f32[25,1,16,256]{3,2,1,0:T(8,128)S(1)}, u32[]{:S(2)}, u32[]{:S(2)}) %collective-permute-start.16) | collective-permute-done | bytes 409632 | tf_op jit(solution)/shard_map/ppermute | solution.py:45
  534.1 4.2 collective-permute-done.17
  (338 shorter events, 48.5 us)
Async XLA Ops:
  0.6 17.2 %copy-start.41 = (f32[16,16,1,1]{1,0,3,2:T(8,128)S(1)}, f32[16,16,1,1]{1,0,3,2:T(8,128)}, u32[]{:S(2)}) copy-start(f32[16,16,1,1]{1,0,3,2:T(8,128)} %constant.314) | copy-start | bytes 3076
  0.6 17.2 %copy-start.13 = (f32[2,16,256]{2,1,0:T(8,128)S(1)}, f32[2,16,256]{2,1,0:T(8,128)}, u32[]{:S(2)}) copy-start(f32[2,16,256]{2,1,0:T(8,128)} %param.21) | copy-start | bytes 98308
  1.7 92.1 %copy-start.22 = (pred[256,8]{1,0:T(8,128)(4,1)}, pred[256,8]{1,0:T(8,128)(4,1)S(1)}, u32[]{:S(2)}) copy-start(pred[256,8]{1,0:T(8,128)(4,1)S(1)} %get-tuple-element.43) | copy-start | bytes 6148
  1.7 17.1 %copy-start.39 = (f32[16,256]{1,0:T(8,128)S(1)}, f32[16,256]{1,0:T(8,128)}, u32[]{:S(2)}) copy-start(f32[16,256]{1,0:T(8,128)} %param.23) | copy-start | bytes 49156
  1.7 17.0 %copy-start.70 = (f32[16,16,1,1]{1,0,3,2:T(8,128)S(1)}, f32[16,16,1,1]{1,0,3,2:T(8,128)}, u32[]{:S(2)}) copy-start(f32[16,16,1,1]{1,0,3,2:T(8,128)} %constant.315) | copy-start | bytes 3076
  2.1 91.7 %copy-start.24 = (pred[256,8]{1,0:T(8,128)(4,1)}, pred[256,8]{1,0:T(8,128)(4,1)S(1)}, u32[]{:S(2)}) copy-start(pred[256,8]{1,0:T(8,128)(4,1)S(1)} %get-tuple-element.46) | copy-start | bytes 6148
  2.1 91.7 %copy-start.26 = (pred[256,8]{1,0:T(8,128)(4,1)}, pred[256,8]{1,0:T(8,128)(4,1)S(1)}, u32[]{:S(2)}) copy-start(pred[256,8]{1,0:T(8,128)(4,1)S(1)} %get-tuple-element.72) | copy-start | bytes 6148
  2.1 91.7 %copy-start.28 = (pred[256,8]{1,0:T(8,128)(4,1)}, pred[256,8]{1,0:T(8,128)(4,1)S(1)}, u32[]{:S(2)}) copy-start(pred[256,8]{1,0:T(8,128)(4,1)S(1)} %get-tuple-element.74) | copy-start | bytes 6148
  2.1 91.7 %copy-start.29 = (pred[256,8]{1,0:T(8,128)(4,1)}, pred[256,8]{1,0:T(8,128)(4,1)S(1)}, u32[]{:S(2)}) copy-start(pred[256,8]{1,0:T(8,128)(4,1)S(1)} %get-tuple-element.76) | copy-start | bytes 6148
  2.1 91.7 %copy-start.30 = (pred[256,8]{1,0:T(8,128)(4,1)}, pred[256,8]{1,0:T(8,128)(4,1)S(1)}, u32[]{:S(2)}) copy-start(pred[256,8]{1,0:T(8,128)(4,1)S(1)} %get-tuple-element.78) | copy-start | bytes 6148
  2.1 91.7 %copy-start.31 = (pred[256,8]{1,0:T(8,128)(4,1)}, pred[256,8]{1,0:T(8,128)(4,1)S(1)}, u32[]{:S(2)}) copy-start(pred[256,8]{1,0:T(8,128)(4,1)S(1)} %get-tuple-element.80) | copy-start | bytes 6148
  2.1 91.7 %copy-start.32 = (pred[256,8]{1,0:T(8,128)(4,1)}, pred[256,8]{1,0:T(8,128)(4,1)S(1)}, u32[]{:S(2)}) copy-start(pred[256,8]{1,0:T(8,128)(4,1)S(1)} %get-tuple-element.82) | copy-start | bytes 6148
  20.7 61.2 %copy-start = (f32[256,53,16]{0,2,1:T(8,128)}, f32[256,53,16]{0,2,1:T(8,128)S(1)}, u32[]{:S(2)}) copy-start(f32[256,53,16]{0,2,1:T(8,128)S(1)} %fusion.59) | copy-start | bytes 2605060
  22.5 195.7 %collective-permute-start.1 = (f32[1,53,16]{0,2,1:T(8,128)}, f32[1,53,16]{0,2,1:T(8,128)}, u32[]{:S(2)}, u32[]{:S(2)}) collective-permute-start(f32[1,53,16]{0,2,1:T(8,128)} %get-tuple-element.62), channel_id=1, source_target_pairs={{28,0},{32,4},{36,8},{40,12},{44,16},{48,20},{52,24},{56,28},{60,3... | collective-permute-start | bytes 10184 | tf_op jit(solution)/shard_map/ppermute | solution.py:18
  68.0 155.5 %collective-permute-start.3 = (f32[1,53,16]{0,2,1:T(8,128)}, f32[1,53,16]{0,2,1:T(8,128)}, u32[]{:S(2)}, u32[]{:S(2)}) collective-permute-start(f32[1,53,16]{0,2,1:T(8,128)} %get-tuple-element.61), channel_id=1, source_target_pairs={{36,0},{40,4},{44,8},{48,12},{52,16},{56,20},{60,24},{64,28},{68,3... | collective-permute-start | bytes 10184 | tf_op jit(solution)/shard_map/ppermute | solution.py:18
  70.0 154.4 %collective-permute-start.4 = (f32[1,53,16]{0,2,1:T(8,128)}, f32[1,53,16]{0,2,1:T(8,128)}, u32[]{:S(2)}, u32[]{:S(2)}) collective-permute-start(f32[1,53,16]{0,2,1:T(8,128)} %get-tuple-element.60), channel_id=1, source_target_pairs={{220,0},{224,4},{228,8},{232,12},{236,16},{240,20},{244,24},{248,2... | collective-permute-start | bytes 10184 | tf_op jit(solution)/shard_map/ppermute | solution.py:18
  78.5 149.6 %collective-permute-start.6 = (f32[1,53,16]{0,2,1:T(8,128)}, f32[1,53,16]{0,2,1:T(8,128)}, u32[]{:S(2)}, u32[]{:S(2)}) collective-permute-start(f32[1,53,16]{0,2,1:T(8,128)} %get-tuple-element.59), channel_id=1, source_target_pairs={{228,0},{232,4},{236,8},{240,12},{244,16},{248,20},{252,24},{0,28}... | collective-permute-start | bytes 10184 | tf_op jit(solution)/shard_map/ppermute | solution.py:18
  81.9 30.0 %copy-start.7 = (f32[256,53,16]{1,2,0:T(8,128)}, f32[256,53,16]{1,2,0:T(8,128)S(1)}, u32[]{:S(2)}) copy-start(f32[256,53,16]{1,2,0:T(8,128)S(1)} %copy.110) | copy-start | bytes 2605060
  83.3 28.6 %copy-start.56 = (pred[16]{0:T(512)(128)(4,1)}, pred[16]{0:T(512)(128)(4,1)S(1)}, u32[]{:S(2)}) copy-start(pred[16]{0:T(512)(128)(4,1)S(1)} %compare_and_fusion.2) | copy-start | bytes 52
  85.6 142.5 %collective-permute-start.5 = (f32[16,53,16]{0,2,1:T(8,128)}, f32[16,53,16]{0,2,1:T(8,128)}, u32[]{:S(2)}, u32[]{:S(2)}) collective-permute-start(f32[16,53,16]{0,2,1:T(8,128)} %broadcast_select_fusion.1), channel_id=1, source_target_pairs={{224,0},{228,4},{232,8},{236,12},{240,16},{244,20},{248,24},{252,2... | collective-permute-start | bytes 162824 | tf_op jit(solution)/shard_map/ppermute | solution.py:18
  141.7 13.9 %copy-start.68 = (pred[256]{0:T(512)(128)(4,1)S(1)}, pred[256]{0:T(512)(128)(4,1)}, u32[]{:S(2)}) copy-start(pred[256]{0:T(512)(128)(4,1)} %get-tuple-element.30) | copy-start | bytes 772
  141.7 14.3 %copy-start.66 = (pred[256]{0:T(512)(128)(4,1)S(1)}, pred[256]{0:T(512)(128)(4,1)}, u32[]{:S(2)}) copy-start(pred[256]{0:T(512)(128)(4,1)} %get-tuple-element.29) | copy-start | bytes 772
  170.1 13.7 %copy-start.64 = (pred[256]{0:T(512)(128)(4,1)S(1)}, pred[256]{0:T(512)(128)(4,1)}, u32[]{:S(2)}) copy-start(pred[256]{0:T(512)(128)(4,1)} %get-tuple-element.28) | copy-start | bytes 772
  197.8 15.1 %copy-start.69 = (s32[16]{0:T(128)S(1)}, s32[16]{0:T(128)}, u32[]{:S(2)}) copy-start(s32[16]{0:T(128)} %compare_select_fusion.5) | copy-start | bytes 196
  197.8 15.1 %copy-start.8 = (f32[256,53,16]{1,2,0:T(8,128)S(1)}, f32[256,53,16]{1,2,0:T(8,128)}, u32[]{:S(2)}) copy-start(f32[256,53,16]{1,2,0:T(8,128)} %copy-done.7) | copy-start | bytes 2605060
  212.9 61.5 %copy-start.38 = (s32[2048]{0:T(1024)}, s32[2048]{0:T(1024)S(1)}, u32[]{:S(2)}) copy-start(s32[2048]{0:T(1024)S(1)} %broadcast_clamp_fusion) | copy-start | bytes 24580
  215.5 52.3 %copy-start.1 = (f32[256,53,16]{0,2,1:T(8,128)S(1)}, f32[256,53,16]{0,2,1:T(8,128)}, u32[]{:S(2)}) copy-start(f32[256,53,16]{0,2,1:T(8,128)} %copy-done) | copy-start | bytes 2605060
  215.5 56.5 %copy-start.50 = (s32[1024]{0:T(1024)}, s32[1024]{0:T(1024)S(1)}, u32[]{:S(2)}) copy-start(s32[1024]{0:T(1024)S(1)} %pad_clamp_fusion.3) | copy-start | bytes 12292
  218.1 43.5 %collective-permute-start.2 = (f32[16,53,16]{0,2,1:T(8,128)S(1)}, f32[16,53,16]{0,2,1:T(8,128)S(1)}, u32[]{:S(2)}, u32[]{:S(2)}) collective-permute-start(f32[16,53,16]{0,2,1:T(8,128)S(1)} %broadcast_select_fusion.2), channel_id=1, source_target_pairs={{32,0},{36,4},{40,8},{44,12},{48,16},{52,20},{56,24},{60,28},{64,3... | collective-permute-start | bytes 162824 | tf_op jit(solution)/shard_map/ppermute | solution.py:18
  223.5 38.2 %collective-permute-start.7 = (f32[16,53,16]{0,2,1:T(8,128)S(1)}, f32[16,53,16]{0,2,1:T(8,128)S(1)}, u32[]{:S(2)}, u32[]{:S(2)}) collective-permute-start(f32[16,53,16]{0,2,1:T(8,128)S(1)} %broadcast_select_fusion), channel_id=1, source_target_pairs={{252,0},{0,4},{4,8},{8,12},{12,16},{16,20},{20,24},{24,28},{28,32}... | collective-permute-start | bytes 162824 | tf_op jit(solution)/shard_map/ppermute | solution.py:18
  224.4 43.4 %collective-permute-start = (f32[16,53,16]{0,2,1:T(8,128)S(1)}, f32[16,53,16]{0,2,1:T(8,128)S(1)}, u32[]{:S(2)}, u32[]{:S(2)}) collective-permute-start(f32[16,53,16]{0,2,1:T(8,128)S(1)} %broadcast_select_fusion.3), channel_id=1, source_target_pairs={{4,0},{8,4},{12,8},{16,12},{20,16},{24,20},{28,24},{32,28},{36,32}... | collective-permute-start | bytes 162824 | tf_op jit(solution)/shard_map/ppermute | solution.py:18
  228.1 82.0 %copy-start.45 = (pred[8,256]{1,0:T(8,128)(4,1)}, pred[8,256]{1,0:T(8,128)(4,1)S(1)}, u32[]{:S(2)}) copy-start(pred[8,256]{1,0:T(8,128)(4,1)S(1)} %copy.109) | copy-start | bytes 6148
  295.1 15.0 %copy-start.10 = (f32[26,2,16,256]{3,2,1,0:T(8,128)S(1)}, f32[26,2,16,256]{3,2,1,0:T(8,128)}, u32[]{:S(2)}) copy-start(f32[26,2,16,256]{3,2,1,0:T(8,128)} %copy-done.9) | copy-start | bytes 2555908
  295.1 15.0 %copy-start.33 = (f32[8,16,16,1]{1,2,0,3:T(8,128)S(1)}, f32[8,16,16,1]{1,2,0,3:T(8,128)}, u32[]{:S(2)}) copy-start(f32[8,16,16,1]{1,2,0,3:T(8,128)} %constant.316) | copy-start | bytes 24580
  295.1 15.0 %copy-start.36 = (f32[1,16,256]{2,1,0:T(8,128)S(1)}, f32[1,16,256]{2,1,0:T(8,128)}, u32[]{:S(2)}) copy-start(f32[1,16,256]{2,1,0:T(8,128)} %copy-done.35) | copy-start | bytes 49156
  325.8 138.3 %collective-permute-start.13 = (f32[16,52,16]{0,2,1:T(8,128)S(1)}, f32[16,52,16]{0,2,1:T(8,128)}, u32[]{:S(2)}, u32[]{:S(2)}) collective-permute-start(f32[16,52,16]{0,2,1:T(8,128)S(1)} %broadcast_select_fusion.5), channel_id=1, source_target_pairs={{224,0},{228,4},{232,8},{236,12},{240,16},{244,20},{248,24},{252,2... | collective-permute-start | bytes 159752 | tf_op jit(solution)/shard_map/ppermute | solution.py:18
  328.1 136.0 %collective-permute-start.15 = (f32[16,52,16]{0,2,1:T(8,128)S(1)}, f32[16,52,16]{0,2,1:T(8,128)}, u32[]{:S(2)}, u32[]{:S(2)}) collective-permute-start(f32[16,52,16]{0,2,1:T(8,128)S(1)} %broadcast_select_fusion.4), channel_id=1, source_target_pairs={{252,0},{0,4},{4,8},{8,12},{12,16},{16,20},{20,24},{24,28},{28,32}... | collective-permute-start | bytes 159752 | tf_op jit(solution)/shard_map/ppermute | solution.py:18
  328.6 49.0 %collective-permute-start.11 = (f32[1,52,16]{0,2,1:T(8,128)}, f32[1,52,16]{0,2,1:T(8,128)S(1)}, u32[]{:S(2)}, u32[]{:S(2)}) collective-permute-start(f32[1,52,16]{0,2,1:T(8,128)} %get-tuple-element.67), channel_id=1, source_target_pairs={{36,0},{40,4},{44,8},{48,12},{52,16},{56,20},{60,24},{64,28},{68,3... | collective-permute-start | bytes 9992 | tf_op jit(solution)/shard_map/ppermute | solution.py:18
  336.2 84.9 %collective-permute-start.12 = (f32[1,52,16]{0,2,1:T(8,128)}, f32[1,52,16]{0,2,1:T(8,128)}, u32[]{:S(2)}, u32[]{:S(2)}) collective-permute-start(f32[1,52,16]{0,2,1:T(8,128)} %get-tuple-element.66), channel_id=1, source_target_pairs={{220,0},{224,4},{228,8},{232,12},{236,16},{240,20},{244,24},{248,2... | collective-permute-start | bytes 9992 | tf_op jit(solution)/shard_map/ppermute | solution.py:18
  339.0 101.4 %collective-permute-start.14 = (f32[1,52,16]{0,2,1:T(8,128)}, f32[1,52,16]{0,2,1:T(8,128)}, u32[]{:S(2)}, u32[]{:S(2)}) collective-permute-start(f32[1,52,16]{0,2,1:T(8,128)} %get-tuple-element.65), channel_id=1, source_target_pairs={{228,0},{232,4},{236,8},{240,12},{244,16},{248,20},{252,24},{0,28}... | collective-permute-start | bytes 9992 | tf_op jit(solution)/shard_map/ppermute | solution.py:18
  377.6 86.5 %collective-permute-start.10 = (f32[16,52,16]{0,2,1:T(8,128)S(1)}, f32[16,52,16]{0,2,1:T(8,128)S(1)}, u32[]{:S(2)}, u32[]{:S(2)}) collective-permute-start(f32[16,52,16]{0,2,1:T(8,128)S(1)} %broadcast_select_fusion.6), channel_id=1, source_target_pairs={{32,0},{36,4},{40,8},{44,12},{48,16},{52,20},{56,24},{60,28},{64,3... | collective-permute-start | bytes 159752 | tf_op jit(solution)/shard_map/ppermute | solution.py:18
  421.1 43.0 %collective-permute-start.9 = (f32[1,52,16]{0,2,1:T(8,128)}, f32[1,52,16]{0,2,1:T(8,128)S(1)}, u32[]{:S(2)}, u32[]{:S(2)}) collective-permute-start(f32[1,52,16]{0,2,1:T(8,128)} %get-tuple-element.68), channel_id=1, source_target_pairs={{28,0},{32,4},{36,8},{40,12},{44,16},{48,20},{52,24},{56,28},{60,3... | collective-permute-start | bytes 9992 | tf_op jit(solution)/shard_map/ppermute | solution.py:18
  440.4 27.8 %collective-permute-start.8 = (f32[16,52,16]{0,2,1:T(8,128)S(1)}, f32[16,52,16]{0,2,1:T(8,128)}, u32[]{:S(2)}, u32[]{:S(2)}) collective-permute-start(f32[16,52,16]{0,2,1:T(8,128)S(1)} %broadcast_select_fusion.7), channel_id=1, source_target_pairs={{4,0},{8,4},{12,8},{16,12},{20,16},{24,20},{28,24},{32,28},{36,32}... | collective-permute-start | bytes 159752 | tf_op jit(solution)/shard_map/ppermute | solution.py:18
  495.6 14.8 %copy-start.34 = (f32[8,16,16,1]{1,2,0,3:T(8,128)S(1)}, f32[8,16,16,1]{1,2,0,3:T(8,128)}, u32[]{:S(2)}) copy-start(f32[8,16,16,1]{1,2,0,3:T(8,128)} %constant.316) | copy-start | bytes 24580
  495.7 14.8 %copy-start.46 = (pred[8,256]{1,0:T(8,128)(4,1)S(1)}, pred[8,256]{1,0:T(8,128)(4,1)}, u32[]{:S(2)}) copy-start(pred[8,256]{1,0:T(8,128)(4,1)} %copy-done.45) | copy-start | bytes 6148
  517.6 9.5 %all-to-all-start = ((f32[4,1,16,256]{3,2,1,0:T(8,128)}), f32[4,1,16,256]{3,2,1,0:T(8,128)S(1)}, u32[]{:S(2)}, u32[]{:S(2)}) async-start(f32[4,1,16,256]{3,2,1,0:T(8,128)} %broadcast_in_dim.123), calls=%async_computation | async-start | bytes 131072 | tf_op jit(solution)/shard_map/all_to_all | solution.py:23
  522.3 11.8 %collective-permute-start.16 = (f32[25,1,16,256]{3,2,1,0:T(8,128)S(1)}, f32[25,1,16,256]{3,2,1,0:T(8,128)S(1)}, u32[]{:S(2)}, u32[]{:S(2)}) collective-permute-start(f32[25,1,16,256]{3,2,1,0:T(8,128)S(1)} %get-tuple-element.70), channel_id=1, source_target_pairs={{0,1},{1,2},{2,3},{4,5},{5,6},{6,7},{8,9},{9,10},{10,11},{12,13},{... | collective-permute-start | bytes 1228808 | tf_op jit(solution)/shard_map/ppermute | solution.py:45
  525.8 12.5 %collective-permute-start.17 = (f32[25,1,16,256]{3,2,1,0:T(8,128)S(1)}, f32[25,1,16,256]{3,2,1,0:T(8,128)S(1)}, u32[]{:S(2)}, u32[]{:S(2)}) collective-permute-start(f32[25,1,16,256]{3,2,1,0:T(8,128)S(1)} %get-tuple-element.69), channel_id=1, source_target_pairs={{1,0},{2,1},{3,2},{5,4},{6,5},{7,6},{9,8},{10,9},{11,10},{13,12},{... | collective-permute-start | bytes 1228808 | tf_op jit(solution)/shard_map/ppermute | solution.py:47
  (43 other events, 262.4 us)
where the time goes:
time: 541 us; the launch traced here: 540 us
  local copies, waits for them, and re-layouts  213 us (39%)
  waiting for transfers between devices  152 us (28%)
  starting transfers between devices  118 us (22%)
  other arithmetic  30.9 us (6%)
  matrix products  15.8 us (3%)
  between operations  10 us (2%)
    ppermute x16, waiting for transfers between devices, shifted(): return lax.ppermute(block, axis, route)  141 us
    ppermute x16, starting transfers between devices, shifted(): return lax.ppermute(block, axis, route)  109 us
    gather x8, local copies, waits for them, and re-layouts, per_device(): positions = jnp.where(relation == peer, start + rank[within], positions)  105 us
    gather x4, local copies, waits for them, and re-layouts, assemble_rows(): picked = jnp.take(extended, flat_index, axis=0).reshape((8,) + rows.shape)  71.3 us
    concatenate x4, local copies, waits for them, and re-layouts, extend(): return jnp.concatenate(pieces, axis=0)  13.2 us
    dot_general x2, matrix products, assemble_rows(): jnp.einsum('dwfm,dmn->wfn', picked, jnp.asarray(link_table()), precision=...  12.1 us
  transfers between devices with their start and end apart: 19, of which 9 were waited for; matrix products, arithmetic and copies ran while one was open for 25% of the time, Pallas kernels for 0%

commit v1 on v0

v1 whole, which is shorter than its diff:
```python
import functools
import math

import jax
import jax.numpy as jnp
import numpy as np
from jax import lax
from jax.experimental import pallas as pl
from jax.experimental.pallas import tpu as pltpu
from jax.sharding import PartitionSpec as P

MESH = pl.DeviceIdType.MESH
PSIDE = 16
ACROSS = 8
NODES = 16
HALF = 128
time_step = 0.035

OPPOSITE = (1, 0, 3, 2, 7, 6, 5, 4)
CORNERS = ((15, 1, 127), (12, 1, 112), (3, 0, 15), (0, 0, 0))


def lagrange_scale(points, which):
    product = 1.0
    for other in range(4):
        if other != which:
            product = product * (points[which] - points[other])
    return product


def node_tables():
    points = np.array([-1.0, -1.0 / math.sqrt(5.0), 1.0 / math.sqrt(5.0), 1.0])
    weights = np.array([1.0, 5.0, 5.0, 1.0]) / 6.0
    derivative = np.zeros((4, 4))
    for target in range(4):
        for source in range(4):
            if target == source:
                derivative[target, source] = sum(
                    1.0 / (points[target] - points[other]) for other in range(4) if other != target
                )
            else:
                derivative[target, source] = lagrange_scale(points, target) / (
                    lagrange_scale(points, source) * (points[target] - points[source])
                )
    return weights, derivative


WEIGHTS, DERIVATIVE = node_tables()
STIFF = WEIGHTS[:, None] * DERIVATIVE


def weighted_difference(f):
    total, gap = f[0] + f[3], f[3] - f[0]
    inner, inner_gap = f[1] + f[2], f[2] - f[1]
    result = [None] * 4
    for i in range(2):
        q = 0.5 * STIFF[i]
        odd = float(q[3] - q[0]) * gap + float(q[2] - q[1]) * inner_gap
        even = float(q[0] + q[3]) * total + float(q[1] + q[2]) * inner
        result[i] = odd + even
        result[3 - i] = odd - even
    return result


def weighted_tendency(h, a, b):
    f = [a[n] * h[n] for n in range(NODES)]
    g = [b[n] * h[n] for n in range(NODES)]
    rows = [weighted_difference(f[4 * j : 4 * j + 4]) for j in range(4)]
    columns = [weighted_difference(g[i::4]) for i in range(4)]
    return [rows[n // 4][n % 4] + columns[n % 4][n // 4] for n in range(NODES)]


def lanes():
    return lax.broadcasted_iota(jnp.int32, (8, HALF), 1)


def sublanes():
    return lax.broadcasted_iota(jnp.int32, (8, HALF), 0)


def roll(x, shift):
    return pltpu.roll(x, (shift + 2 * HALF) % HALF, 1)


def assembled_in_patch(v):
    lane = lanes()
    column = lane % PSIDE
    for half in range(2):
        for j in range(4):
            left, right = v[half][4 * j], v[half][4 * j + 3]
            v[half][4 * j + 3] = right + jnp.where(column < PSIDE - 1, roll(left, -1), 0.0)
            v[half][4 * j] = left + jnp.where(column > 0, roll(right, 1), 0.0)
    edge = HALF - PSIDE
    for i in range(4):
        low = [v[0][i], v[1][i]]
        high = [v[0][12 + i], v[1][12 + i]]
        down = [roll(low[0], -PSIDE), roll(low[1], -PSIDE)]
        up = [roll(high[0], PSIDE), roll(high[1], PSIDE)]
        v[0][12 + i] = high[0] + jnp.where(lane < edge, down[0], down[1])
        v[1][12 + i] = high[1] + jnp.where(lane < edge, down[1], 0.0)
        v[0][i] = low[0] + jnp.where(lane >= PSIDE, up[0], 0.0)
        v[1][i] = low[1] + jnp.where(lane >= PSIDE, up[1], up[0])
    return v


def pack_borders(v, q, send, corners):
    lane, sub = lanes(), sublanes()
    column, block = lane % PSIDE, lane // PSIDE
    group, slot = q // 4, q % 4
    for half in range(2):
        east = west = 0.0
        for j in range(4):
            at = 4 * slot + j
            east = east + jnp.where(column == at, roll(v[half][4 * j + 3], at - (PSIDE - 1)), 0.0)
            west = west + jnp.where(column == at, roll(v[half][4 * j], at), 0.0)
        send[0, group, half] += east
        send[1, group, half] += west
    north = south = 0.0
    for i in range(4):
        at = 4 * (slot % 2) + i
        north = north + jnp.where(
            block == at, roll(v[1][12 + i], PSIDE * at - (HALF - PSIDE)), 0.0
        )
        south = south + jnp.where(block == at, roll(v[0][i], PSIDE * at), 0.0)
    send[2, group, slot // 2] += north
    send[3, group, slot // 2] += south
    result = []
    for k, (node, half, where) in enumerate(CORNERS):
        value = jnp.broadcast_to(v[half][node][:, where : where + 1], (8, HALF))
        result.append(corners[k] + jnp.where(lane == 8 * q + sub, value, 0.0))
    return tuple(result)


def add_borders(v, q, lines, corners):
    lane, sub = lanes(), sublanes()
    column = lane % PSIDE
    group, slot = q // 4, q % 4
    for half in range(2):
        from_east, from_west = lines[0, group, half], lines[1, group, half]
        for j in range(4):
            at = 4 * slot + j
            v[half][4 * j + 3] += jnp.where(
                column == PSIDE - 1, roll(from_east, PSIDE - 1 - at), 0.0
            )
            v[half][4 * j] += jnp.where(column == 0, roll(from_west, -at), 0.0)
    from_north, from_south = lines[2, group, slot // 2], lines[3, group, slot // 2]
    for i in range(4):
        at = 4 * (slot % 2) + i
        v[1][12 + i] += jnp.where(
            lane >= HALF - PSIDE, roll(from_north, HALF - PSIDE - PSIDE * at), 0.0
        )
        v[0][i] += jnp.where(lane < PSIDE, roll(from_south, -PSIDE * at), 0.0)
    for k, (node, half, where) in enumerate(CORNERS):
        row = jnp.broadcast_to(corners[k], (8, HALF))
        value = jnp.sum(jnp.where(lane == 8 * q + sub, row, 0.0), axis=1, keepdims=True)
        v[half][node] += jnp.where(lane == where, value, 0.0)
    return v


def permuted(x, table):
    high = x.astype(jnp.bfloat16)
    rest = x - high.astype(jnp.float32)
    middle = rest.astype(jnp.bfloat16)
    low = (rest - middle.astype(jnp.float32)).astype(jnp.bfloat16)
    dot = functools.partial(jnp.dot, preferred_element_type=jnp.float32)
    return dot(high, table) + dot(middle, table) + dot(low, table)


def halves(x):
    return [x[:, :HALF], x[:, HALF:]]


def kernel(
    n_elem,
    n_lev,
    trc,
    thickness,
    winds,
    metric,
    beside,
    out,
    surf,
    near,
    raw,
    small_raw,
    small,
    tables,
    state,
    rate,
    coef,
    mixed_coef,
    mass,
    shared,
    scale,
    line_send,
    line_recv,
    corner_send,
    corner_recv,
    thick,
    last,
    inverse,
    column,
    columns,
    ratio,
    ratio_recv,
    last_ratio,
    last_recv,
    delta,
    result,
    last_rows,
    in_sem,
    small_sem,
    out_sem,
    line_ssem,
    line_rsem,
    column_ssem,
    column_rsem,
    ratio_ssem,
    ratio_rsem,
):
    place, level = lax.axis_index("elem"), lax.axis_index("lev")
    width = 2 * HALF
    offsets = (
        1,
        -1,
        ACROSS,
        -ACROSS,
        ACROSS + 1,
        ACROSS - 1,
        1 - ACROSS,
        -1 - ACROSS,
    )
    targets = [{"elem": lax.rem(place + offset + n_elem, n_elem)} for offset in offsets]
    peers = [{"lev": lax.rem(level + k, n_lev)} for k in range(1, n_lev)]

    barrier = pltpu.get_barrier_semaphore()
    for target in targets + peers:
        pl.semaphore_signal(barrier, inc=1, device_id=target, device_id_type=MESH)

    near_copy = pltpu.make_async_copy(beside, near, small_sem.at[0])
    near_copy.start()
    pieces = [
        (trc.at[pl.ds(768, 32)], 0, 32),
        (thickness, 32, 32),
        (winds, 64, 64),
        (metric, 128, 16),
    ]
    small_copies = []
    for k, (source, start, size) in enumerate(pieces):
        copy = pltpu.make_async_copy(
            source, small_raw.at[pl.ds(start, size)], small_sem.at[k + 1]
        )
        copy.start()
        small_copies.append(copy)
    in_copies = []
    for half in range(2):
        copy = pltpu.make_async_copy(
            trc.at[pl.ds(0, 768), pl.ds(HALF * half, HALF)], raw.at[half], in_sem.at[half]
        )
        copy.start()
        in_copies.append(copy)

    line_send[...] = jnp.zeros_like(line_send)

    @pl.when(level == 0)
    def _():
        ratio_recv[:, 1] = jnp.zeros_like(ratio_recv[:, 1])
        last_recv[1] = jnp.zeros_like(last_recv[1])

    @pl.when(level == n_lev - 1)
    def _():
        ratio_recv[:, 0] = jnp.zeros_like(ratio_recv[:, 0])
        last_recv[0] = jnp.zeros_like(last_recv[0])

    near_copy.wait()
    dot = functools.partial(jnp.dot, preferred_element_type=jnp.float32)
    element = lax.broadcasted_iota(jnp.int32, (width, width), 0)
    own = near[...] - place * width
    spots = []
    for side in (1, 3):
        step = jnp.where(own[side : side + 1, :] == element, 1.0, 0.0).astype(jnp.bfloat16)
        count = dot(jnp.ones((8, width), jnp.bfloat16), step)
        for doubling in range(4):
            count = count + dot(count.astype(jnp.bfloat16), step)
            if doubling < 3:
                step = dot(step, step).astype(jnp.bfloat16)
        spots.append(count)
    spot = (spots[0] + PSIDE * spots[1]).astype(jnp.int32)[0:1, :]
    to_drawn = jnp.where(spot == element, 1.0, 0.0)
    tables[1] = to_drawn.astype(jnp.bfloat16)
    tables[0] = jnp.transpose(to_drawn).astype(jnp.bfloat16)

    for copy in small_copies:
        copy.wait()
    small[...] = permuted(small_raw[...], tables[0])
    node = lax.broadcasted_iota(jnp.int32, (NODES, width), 0)
    point_i, point_j = node % 4, node // 4
    ends, inside = float(WEIGHTS[0]), float(WEIGHTS[1])
    weight_i = jnp.where((point_i == 0) | (point_i == 3), ends, inside)
    weight_j = jnp.where((point_j == 0) | (point_j == 3), ends, inside)
    area = small[pl.ds(128, NODES), :]
    mass[...] = weight_i * weight_j * area
    for l in range(2):
        coef[0, l] = -(weight_j * area) * small[pl.ds(64 + 16 * l, NODES), :]
        coef[1, l] = -(weight_i * area) * small[pl.ds(96 + 16 * l, NODES), :]

    for copy in in_copies:
        copy.wait()

    def take_in(q, carry):
        t, l = q // 2, q % 2
        x = jnp.concatenate(
            [
                jnp.concatenate(
                    [
                        raw[half, pl.ds(256 * t + 16 * l + n, 8, stride=32), :]
                        for n in range(NODES)
                    ],
                    axis=0,
                )
                for half in range(2)
            ],
            axis=1,
        )
        y = permuted(x, tables[0])
        for n in range(NODES):
            layer = small[pl.ds(32 + 16 * l + n, 1), :]
            state[q, n] = y[8 * n : 8 * n + 8] * layer
        return carry

    lax.fori_loop(0, 6, take_in, 0, unroll=True)
    wide_sub = lax.broadcasted_iota(jnp.int32, (8, width), 0)
    for n in range(NODES):
        tile = jnp.zeros((8, width), jnp.float32)
        for l in range(2):
            layer = small[pl.ds(32 + 16 * l + n, 1), :]
            tile = jnp.where(wide_sub == 2 * l, small[pl.ds(16 * l + n, 1), :] * layer, tile)
            tile = jnp.where(wide_sub == 2 * l + 1, layer, tile)
        state[6, n] = tile
        for k in range(2):
            mixed_coef[k, n] = jnp.where(
                wide_sub < 2, coef[k, 0, pl.ds(n, 1), :], coef[k, 1, pl.ds(n, 1), :]
            )

    def level_coef(l, half):
        at = pl.ds(HALF * half, HALF)
        return [[coef[k, l, pl.ds(n, 1), at] for n in range(NODES)] for k in range(2)]

    def both_coef(half):
        at = pl.ds(HALF * half, HALF)
        return [[mixed_coef[k, n, :, at] for n in range(NODES)] for k in range(2)]

    def load(ref, q):
        return [
            [ref[q, n, :, pl.ds(HALF * half, HALF)] for n in range(NODES)] for half in range(2)
        ]

    def save(ref, q, v):
        for half in range(2):
            for n in range(NODES):
                ref[q, n, :, pl.ds(HALF * half, HALF)] = v[half][n]

    def scaled(half):
        at = pl.ds(HALF * half, HALF)
        return [scale[pl.ds(n, 1), at] for n in range(NODES)]

    def tend(q, h, stage, corners, mixed):
        v = []
        for half in range(2):
            a, b = both_coef(half) if mixed else level_coef(q % 2, half)
            rates = weighted_tendency(h[half], a, b)
            if mixed:
                at = pl.ds(HALF * half, HALF)
                rates = [
                    jnp.where(sublanes() == 4, mass[pl.ds(n, 1), at], rates[n])
                    for n in range(NODES)
                ]
            v.append(rates)
        v = assembled_in_patch(v)
        save(rate, q, v)
        return pack_borders(v, q, line_send.at[stage], corners)

    def exchange(stage):
        copies = []
        for side, target in enumerate(targets):
            if side < 4:
                source = line_send.at[stage, side]
                landing = line_recv.at[stage, OPPOSITE[side]]
            else:
                source = corner_send.at[stage, side - 4]
                landing = corner_recv.at[stage, OPPOSITE[side] - 4]
            copy = pltpu.make_async_remote_copy(
                src_ref=source,
                dst_ref=landing,
                send_sem=line_ssem.at[stage, side],
                recv_sem=line_rsem.at[stage, OPPOSITE[side]],
                device_id=target,
                device_id_type=MESH,
            )
            copy.start()
            copies.append(copy)
        return copies

    def put_corners(stage, corners):
        for k in range(4):
            corner_send[stage, k] = jnp.sum(corners[k], axis=0, keepdims=True)

    def complete(q, stage):
        borders = [corner_recv[stage, k] for k in range(4)]
        return add_borders(load(rate, q), q, line_recv.at[stage], borders)

    no_corners = tuple(jnp.zeros((8, HALF), jnp.float32) for _ in range(4))

    corners = lax.fori_loop(
        0, 6, lambda q, c: tend(q, load(state, q), 0, c, False), no_corners, unroll=True
    )
    corners = tend(6, load(state, 6), 0, corners, True)
    put_corners(0, corners)
    pl.semaphore_wait(barrier, len(targets) + len(peers))
    sends = exchange(0)
    for copy in sends:
        copy.wait_recv()

    v = complete(6, 0)
    for half in range(2):
        for n in range(NODES):
            shared[pl.ds(n, 1), pl.ds(HALF * half, HALF)] = v[half][n][4:5, :]
    scale[...] = time_step / shared[...]

    def advance(q, v, corners, mixed):
        h = load(state, q)
        for half in range(2):
            c = scaled(half)
            for n in range(NODES):
                middle = h[half][n] + c[n] * v[half][n]
                state[q, n, :, pl.ds(HALF * half, HALF)] = h[half][n] + middle
                h[half][n] = middle
        return tend(q, h, 1, corners, mixed)

    corners = advance(6, v, no_corners, True)
    corners = lax.fori_loop(
        0, 6, lambda q, c: advance(q, complete(q, 0), c, False), corners, unroll=True
    )
    put_corners(1, corners)
    second_sends = exchange(1)
    for copy in second_sends:
        copy.wait_recv()

    def finish(q):
        v = complete(q, 1)
        h = load(state, q)
        for half in range(2):
            c = scaled(half)
            for n in range(NODES):
                h[half][n] = 0.5 * (h[half][n] + c[n] * v[half][n])
        return h

    h = finish(6)
    for half in range(2):
        at = pl.ds(HALF * half, HALF)
        for n in range(NODES):
            for l in range(2):
                last[l, pl.ds(n, 1), at] = h[half][n][2 * l : 2 * l + 1, :]
                thick[l, pl.ds(n, 1), at] = h[half][n][2 * l + 1 : 2 * l + 2, :]
    column[...] = thick[0] + thick[1]
    column_copies = []
    for k, peer in enumerate(peers):
        copy = pltpu.make_async_remote_copy(
            src_ref=column,
            dst_ref=columns.at[k],
            send_sem=column_ssem.at[k],
            recv_sem=column_rsem.at[k],
            device_id=peer,
            device_id_type=MESH,
        )
        copy.start()
        column_copies.append(copy)

    below = {"lev": lax.rem(level + n_lev - 1, n_lev)}
    above = {"lev": lax.rem(level + 1, n_lev)}

    def ratio_copy(t, l):
        return pltpu.make_async_remote_copy(
            src_ref=last_ratio.at[l] if t == 3 else ratio.at[t, l],
            dst_ref=last_recv.at[l] if t == 3 else ratio_recv.at[t, l],
            send_sem=ratio_ssem.at[t, l],
            recv_sem=ratio_rsem.at[t, l],
            device_id=below if l == 0 else above,
            device_id_type=MESH,
        )

    has_below, has_above = level > 0, level < n_lev - 1

    def send_ratios(t):
        pl.when(has_below)(lambda: ratio_copy(t, 0).start())
        pl.when(has_above)(lambda: ratio_copy(t, 1).start())

    for l in range(2):
        inverse[l] = 1.0 / thick[l]
        last_ratio[l] = last[l] * inverse[l]
    send_ratios(3)

    for t in range(3):

        def edge(l, carry, t=t):
            q = 2 * t + l
            h = finish(q)
            for half in range(2):
                at = pl.ds(HALF * half, HALF)
                for n in range(NODES):
                    state[q, n, :, at] = h[half][n]
                    ratio[t, l, n, :, at] = h[half][n] * inverse[l, pl.ds(n, 1), at]
            return carry

        lax.fori_loop(0, 2, edge, 0, unroll=True)
        send_ratios(t)

    for copy in column_copies:
        copy.wait_recv()
    own_column = column[...]
    total = own_column
    under = jnp.zeros_like(own_column)
    for k in range(1, n_lev):
        part = columns[k - 1]
        total = total + part
        under = under + jnp.where(k <= level, part, 0.0)
    surface_rows = total
    levels = 2 * n_lev

    def as_float(k):
        return k.astype(jnp.float32)

    for k in range(3):
        edge_level = as_float(2 * level + k)
        fraction = (edge_level + edge_level * (edge_level - 1.0) * (1.0 / (levels - 1))) * (
            0.5 / levels
        )
        if k > 0:
            under = under + thick[k - 1]
        delta[k] = under - surface_rows * fraction
    for l in range(2):
        share = (1.0 + 2.0 * as_float(2 * level + l) * (1.0 / (levels - 1))) * (0.5 / levels)
        delta[3 + l] = 1.0 / (surface_rows * share)

    def wait_ratios(t):
        pl.when(has_above)(lambda: ratio_copy(t, 0).wait_recv())
        pl.when(has_below)(lambda: ratio_copy(t, 1).wait_recv())

    def remapped(d, carried, own_ratio, ratio_above, ratio_below):
        low = d[0] * jnp.where(d[0] > 0.0, ratio_below, own_ratio[0])
        middle = d[1] * jnp.where(d[1] > 0.0, own_ratio[0], own_ratio[1])
        high = d[2] * jnp.where(d[2] > 0.0, own_ratio[1], ratio_above)
        return (carried[0] + low - middle) * d[3], (carried[1] + middle - high) * d[4]

    wait_ratios(3)
    d = [delta[k] for k in range(5)]
    first, second = remapped(
        d, [last[0], last[1]], [last_ratio[0], last_ratio[1]], last_recv[0], last_recv[1]
    )
    rows = permuted(jnp.concatenate([first, second, surface_rows], axis=0), tables[1])
    last_rows[...] = rows
    out_copies = [
        pltpu.make_async_copy(last_rows.at[pl.ds(32, 16)], surf, out_sem.at[3, 0]),
        pltpu.make_async_copy(
            last_rows.at[pl.ds(0, 32)], out.at[pl.ds(768, 32)], out_sem.at[3, 1]
        ),
    ]
    for copy in out_copies:
        copy.start()

    for t in range(3):
        wait_ratios(t)
        pairs = []
        for n in range(NODES):
            d = [delta[k, pl.ds(n, 1), :] for k in range(5)]
            pairs.append(
                remapped(
                    d,
                    [state[2 * t, n], state[2 * t + 1, n]],
                    [ratio[t, 0, n], ratio[t, 1, n]],
                    ratio_recv[t, 0, n],
                    ratio_recv[t, 1, n],
                )
            )
        for l in range(2):
            tiles = permuted(jnp.concatenate([pair[l] for pair in pairs], axis=0), tables[1])
            for n in range(NODES):
                for half in range(2):
                    result[half, pl.ds(256 * t + 16 * l + n, 8, stride=32), :] = tiles[
                        8 * n : 8 * n + 8, HALF * half : HALF * half + HALF
                    ]
        rows = pl.ds(256 * t, 256)
        for half in range(2):
            copy = pltpu.make_async_copy(
                result.at[half, rows],
                out.at[rows, pl.ds(HALF * half, HALF)],
                out_sem.at[t, half],
            )
            copy.start()
            out_copies.append(copy)

    for copy in out_copies:
        copy.wait()
    for copy in sends + second_sends + column_copies:
        copy.wait_send()
    for t in range(4):
        pl.when(has_below)(lambda t=t: ratio_copy(t, 0).wait_send())
        pl.when(has_above)(lambda t=t: ratio_copy(t, 1).wait_send())


def per_device(n_elem, n_lev, tracers, layer_mass, winds, metric, neighbours):
    width = metric.shape[-1]
    f32 = jnp.float32
    any_spec = pl.BlockSpec(memory_space=pl.ANY)
    tile = (NODES, 8, width)
    dma = pltpu.SemaphoreType.DMA
    scratch = [
        pltpu.VMEM((8, width), jnp.int32),
        pltpu.VMEM((2, 768, HALF), f32),
        pltpu.VMEM((144, width), f32),
        pltpu.VMEM((144, width), f32),
        pltpu.VMEM((2, width, width), jnp.bfloat16),
        pltpu.VMEM((7,) + tile, f32),
        pltpu.VMEM((7,) + tile, f32),
        pltpu.VMEM((2, 2, NODES, width), f32),
        pltpu.VMEM((2,) + tile, f32),
        pltpu.VMEM((NODES, width), f32),
        pltpu.VMEM((NODES, width), f32),
        pltpu.VMEM((NODES, width), f32),
        pltpu.VMEM((2, 4, 2, 2, 8, HALF), f32),
        pltpu.VMEM((2, 4, 2, 2, 8, HALF), f32),
        pltpu.VMEM((2, 4, 1, HALF), f32),
        pltpu.VMEM((2, 4, 1, HALF), f32),
        pltpu.VMEM((2, NODES, width), f32),
        pltpu.VMEM((2, NODES, width), f32),
        pltpu.VMEM((2, NODES, width), f32),
        pltpu.VMEM((NODES, width), f32),
        pltpu.VMEM((n_lev - 1, NODES, width), f32),
        pltpu.VMEM((3, 2) + tile, f32),
        pltpu.VMEM((3, 2) + tile, f32),
        pltpu.VMEM((2, NODES, width), f32),
        pltpu.VMEM((2, NODES, width), f32),
        pltpu.VMEM((5, NODES, width), f32),
        pltpu.VMEM((2, 768, HALF), f32),
        pltpu.VMEM((3 * NODES, width), f32),
        dma((2,)),
        dma((5,)),
        dma((4, 2)),
        dma((2, 8)),
        dma((2, 8)),
        dma((n_lev - 1,)),
        dma((n_lev - 1,)),
        dma((4, 2)),
        dma((4, 2)),
    ]
    out, surface = pl.pallas_call(
        functools.partial(kernel, n_elem, n_lev),
        out_shape=(
            jax.ShapeDtypeStruct((800, width), f32),
            jax.ShapeDtypeStruct((NODES, width), f32),
        ),
        in_specs=[any_spec] * 5,
        out_specs=(any_spec, any_spec),
        scratch_shapes=scratch,
        compiler_params=pltpu.CompilerParams(collective_id=0, has_side_effects=True),
        name="transport",
    )(
        tracers.reshape(-1, width),
        layer_mass.reshape(-1, width),
        winds.reshape(-1, width),
        metric,
        jnp.transpose(neighbours),
    )
    return out.reshape(tracers.shape), surface


def solution(mesh):
    placed = (
        P(None, "lev", None, ("members", "elem")),
        P("lev", None, ("members", "elem")),
        P(None, "lev", None, ("members", "elem")),
        P(None, "elem"),
        P("elem", None),
    )
    return jax.shard_map(
        functools.partial(per_device, mesh.shape["elem"], mesh.shape["lev"]),
        mesh=mesh,
        in_specs=placed,
        out_specs=(P(None, "lev", None, ("members", "elem")), P(None, ("members", "elem"))),
        check_vma=False,
    )
```

time: 541 us -> 77.1 us (0.14)
  local copies, waits for them, and re-layouts: 213 us -> 2.73 us
  waiting for transfers between devices: 152 us -> 0 us
  starting transfers between devices: 118 us -> 0 us
  Pallas kernels: 0 us -> 73.6 us
  other arithmetic: 30.9 us -> 0 us
  matrix products: 15.8 us -> 0 us
  between operations: 10 us -> 0.65 us
    gather x28 -> x0, local copies, waits for them, and re-layouts: 185 us -> none  [the longest x8 105 us: per_device(): positions = jnp.where(relation == peer, start + rank[within], positions)]
    ppermute x18 -> x0, waiting for transfers between devices: 152 us -> none  [the longest x16 141 us: shifted(): return lax.ppermute(block, axis, route)]
    ppermute x18 -> x0, starting transfers between devices: 114 us -> none  [the longest x16 109 us: shifted(): return lax.ppermute(block, axis, route)]
    pallas_call x0 -> x1, Pallas kernels: none -> 73.6 us  [per_device(): pl.pallas_call(functools.partial(kernel, n_elem, n_lev), out_shape=(jax.S...]
    dot_general x6 -> x0, matrix products: 15.8 us -> none  [the longest x2 12.1 us: assemble_rows(): jnp.einsum('dwfm,dmn->wfn', picked, jnp.asarray(link_table()), precision=...]
    concatenate x4 -> x0, local copies, waits for them, and re-layouts: 13.2 us -> none  [extend(): return jnp.concatenate(pieces, axis=0)]
    select_n x15 -> x0, other arithmetic: 7.4 us -> none  [the longest x13 7.33 us: extend(): packed = jnp.take(rows, order, axis=0)]
    another operation x33 -> x0, other arithmetic: 5.59 us -> none
  transfers between devices with their start and end apart: 19 -> 0, of which waited for: 9 -> 0; matrix products, arithmetic and copies ran while one was open for 25% -> 0% of each run, Pallas kernels for 0% -> 0%
where the time goes in v1:
time: 77.1 us; the launch traced here: 77 us
  Pallas kernels  73.6 us (95%)
  local copies, waits for them, and re-layouts  2.73 us (4%)
    pallas_call x1, Pallas kernels, per_device(): pl.pallas_call(functools.partial(kernel, n_elem, n_lev), out_shape=(jax.S...  73.6 us
    unnamed x4, local copies, waits for them, and re-layouts  2.73 us

profile of v1, /device:TPU:33, one launch (start us, length us, event | category | flops | bytes accessed | tf_op | source)
XLA Modules:
  0.0 77.0 jit_solution(12009550404456647358)
XLA Ops:
  0.6 73.6 %transport.1 = (f32[800,256]{1,0:T(8,128)}, f32[16,256]{1,0:T(8,128)}) custom-call(f32[800,256]{1,0:T(8,128)} %bitcast.5, f32[32,256]{1,0:T(8,128)} %bitcast.8, f32[64,256]{1,0:T(8,128)} %bitcast.7, f32[16,256]{1,0:T(8,128)} %metric.1, s32[8,256]{1,0:T(8,128)} %bitcast.9), custom_call_target="tpu_custom_call" | custom-call | tf_op jit(solution)/shard_map/transport/pallas_call | solution.py:656
  74.2 0.0 copy-start
  74.2 2.1 %copy.9 = f32[25,2,16,256]{3,2,1,0:T(8,128)} copy(f32[25,2,16,256]{3,2,1,0:T(8,128)} %bitcast.6) | data formatting | bytes 1638400
  76.4 0.0 copy-done
  76.4 0.6 copy.10
Async XLA Ops:
  74.2 2.1 %copy-start = (f32[16,256]{1,0:T(8,128)S(1)}, f32[16,256]{1,0:T(8,128)}, u32[]{:S(2)}) copy-start(f32[16,256]{1,0:T(8,128)} %get-tuple-element.9) | copy-start | bytes 49156

commit v2 on v1

--- a/solution.py
+++ b/solution.py
@@ -103,18 +103,17 @@
     return v
 
 
-def pack_borders(v, q, send, corners):
-    lane, sub = lanes(), sublanes()
+def lines_of(v, slot):
+    lane = lanes()
     column, block = lane % PSIDE, lane // PSIDE
-    group, slot = q // 4, q % 4
+    found = []
     for half in range(2):
         east = west = 0.0
         for j in range(4):
             at = 4 * slot + j
             east = east + jnp.where(column == at, roll(v[half][4 * j + 3], at - (PSIDE - 1)), 0.0)
             west = west + jnp.where(column == at, roll(v[half][4 * j], at), 0.0)
-        send[0, group, half] += east
-        send[1, group, half] += west
+        found += [(0, half, east), (1, half, west)]
     north = south = 0.0
     for i in range(4):
         at = 4 * (slot % 2) + i
@@ -122,39 +121,50 @@
             block == at, roll(v[1][12 + i], PSIDE * at - (HALF - PSIDE)), 0.0
         )
         south = south + jnp.where(block == at, roll(v[0][i], PSIDE * at), 0.0)
-    send[2, group, slot // 2] += north
-    send[3, group, slot // 2] += south
+    return found + [(2, slot // 2, north), (3, slot // 2, south)]
+
+
+def corners_of(v, slot, corners):
+    lane, sub = lanes(), sublanes()
     result = []
     for k, (node, half, where) in enumerate(CORNERS):
         value = jnp.broadcast_to(v[half][node][:, where : where + 1], (8, HALF))
-        result.append(corners[k] + jnp.where(lane == 8 * q + sub, value, 0.0))
+        result.append(corners[k] + jnp.where(lane == 8 * slot + sub, value, 0.0))
     return tuple(result)
 
 
-def add_borders(v, q, lines, corners):
-    lane, sub = lanes(), sublanes()
+def placed_lines(slot, lines):
+    lane = lanes()
     column = lane % PSIDE
-    group, slot = q // 4, q % 4
+    found = []
     for half in range(2):
-        from_east, from_west = lines[0, group, half], lines[1, group, half]
+        east, west = lines[0, half], lines[1, half]
         for j in range(4):
             at = 4 * slot + j
-            v[half][4 * j + 3] += jnp.where(
-                column == PSIDE - 1, roll(from_east, PSIDE - 1 - at), 0.0
-            )
-            v[half][4 * j] += jnp.where(column == 0, roll(from_west, -at), 0.0)
-    from_north, from_south = lines[2, group, slot // 2], lines[3, group, slot // 2]
+            found.append((half, 4 * j + 3, column == PSIDE - 1, roll(east, PSIDE - 1 - at)))
+            found.append((half, 4 * j, column == 0, roll(west, -at)))
+    north, south = lines[2, slot // 2], lines[3, slot // 2]
     for i in range(4):
         at = 4 * (slot % 2) + i
-        v[1][12 + i] += jnp.where(
-            lane >= HALF - PSIDE, roll(from_north, HALF - PSIDE - PSIDE * at), 0.0
-        )
-        v[0][i] += jnp.where(lane < PSIDE, roll(from_south, -PSIDE * at), 0.0)
+        found.append(
+            (1, 12 + i, lane >= HALF - PSIDE, roll(north, HALF - PSIDE - PSIDE * at))
+        )
+        found.append((0, i, lane < PSIDE, roll(south, -PSIDE * at)))
+    return found
+
+
+def borders_of(slot, lines, corners):
+    lane, sub = lanes(), sublanes()
+    extra = [{}, {}]
+    found = placed_lines(slot, lines)
     for k, (node, half, where) in enumerate(CORNERS):
         row = jnp.broadcast_to(corners[k], (8, HALF))
-        value = jnp.sum(jnp.where(lane == 8 * q + sub, row, 0.0), axis=1, keepdims=True)
-        v[half][node] += jnp.where(lane == where, value, 0.0)
-    return v
+        value = jnp.sum(jnp.where(lane == 8 * slot + sub, row, 0.0), axis=1, keepdims=True)
+        found.append((half, node, lane == where, value))
+    for half, node, mask, value in found:
+        part = jnp.where(mask, value, 0.0)
+        extra[half][node] = extra[half][node] + part if node in extra[half] else part
+    return extra
 
 
 def permuted(x, table):
@@ -205,6 +215,8 @@
     ratio_recv,
     last_ratio,
     last_recv,
+    edge_send,
+    edge_recv,
     delta,
     result,
     last_rows,
@@ -217,6 +229,8 @@
     column_rsem,
     ratio_ssem,
     ratio_rsem,
+    edge_ssem,
+    edge_rsem,
 ):
     place, level = lax.axis_index("elem"), lax.axis_index("lev")
     width = 2 * HALF
@@ -261,14 +275,17 @@
         in_copies.append(copy)
 
     line_send[...] = jnp.zeros_like(line_send)
+    edge_send[...] = jnp.zeros_like(edge_send)
 
     @pl.when(level == 0)
     def _():
+        edge_recv[1] = jnp.zeros_like(edge_recv[1])
         ratio_recv[:, 1] = jnp.zeros_like(ratio_recv[:, 1])
         last_recv[1] = jnp.zeros_like(last_recv[1])
 
     @pl.when(level == n_lev - 1)
     def _():
+        edge_recv[0] = jnp.zeros_like(edge_recv[0])
         ratio_recv[:, 0] = jnp.zeros_like(ratio_recv[:, 0])
         last_recv[0] = jnp.zeros_like(last_recv[0])
 
@@ -308,7 +325,7 @@
         copy.wait()
 
     def take_in(q, carry):
-        t, l = q // 2, q % 2
+        t, l = (q - 1) // 2, (q - 1) % 2
         x = jnp.concatenate(
             [
                 jnp.concatenate(
@@ -328,7 +345,7 @@
             state[q, n] = y[8 * n : 8 * n + 8] * layer
         return carry
 
-    lax.fori_loop(0, 6, take_in, 0, unroll=True)
+    lax.fori_loop(1, 7, take_in, 0, unroll=True)
     wide_sub = lax.broadcasted_iota(jnp.int32, (8, width), 0)
     for n in range(NODES):
         tile = jnp.zeros((8, width), jnp.float32)
@@ -336,7 +353,7 @@
             layer = small[pl.ds(32 + 16 * l + n, 1), :]
             tile = jnp.where(wide_sub == 2 * l, small[pl.ds(16 * l + n, 1), :] * layer, tile)
             tile = jnp.where(wide_sub == 2 * l + 1, layer, tile)
-        state[6, n] = tile
+        state[0, n] = tile
         for k in range(2):
             mixed_coef[k, n] = jnp.where(
                 wide_sub < 2, coef[k, 0, pl.ds(n, 1), :], coef[k, 1, pl.ds(n, 1), :]
@@ -364,10 +381,10 @@
         at = pl.ds(HALF * half, HALF)
         return [scale[pl.ds(n, 1), at] for n in range(NODES)]
 
-    def tend(q, h, stage, corners, mixed):
+    def rates_of(q, h, mixed):
         v = []
         for half in range(2):
-            a, b = both_coef(half) if mixed else level_coef(q % 2, half)
+            a, b = both_coef(half) if mixed else level_coef((q - 1) % 2, half)
             rates = weighted_tendency(h[half], a, b)
             if mixed:
                 at = pl.ds(HALF * half, HALF)
@@ -376,108 +393,62 @@
                     for n in range(NODES)
                 ]
             v.append(rates)
-        v = assembled_in_patch(v)
-        save(rate, q, v)
-        return pack_borders(v, q, line_send.at[stage], corners)
-
-    def exchange(stage):
+        return assembled_in_patch(v)
+
+    def pack(v, q, stage, group, corners):
+        slot = q - 4 * group
+        for side, half, value in lines_of(v, slot):
+            line_send[stage, group, side, half] += value
+        return corners_of(v, slot, corners)
+
+    def exchange(stage, group, corners):
+        for k in range(4):
+            corner_send[stage, group, k] = jnp.sum(corners[k], axis=0, keepdims=True)
         copies = []
-        for side, target in enumerate(targets):
+        for side in (2, 3, 4, 5, 6, 7, 0, 1):
             if side < 4:
-                source = line_send.at[stage, side]
-                landing = line_recv.at[stage, OPPOSITE[side]]
+                source = line_send.at[stage, group, side]
+                landing = line_recv.at[stage, group, OPPOSITE[side]]
             else:
-                source = corner_send.at[stage, side - 4]
-                landing = corner_recv.at[stage, OPPOSITE[side] - 4]
+                source = corner_send.at[stage, group, side - 4]
+                landing = corner_recv.at[stage, group, OPPOSITE[side] - 4]
             copy = pltpu.make_async_remote_copy(
                 src_ref=source,
                 dst_ref=landing,
-                send_sem=line_ssem.at[stage, side],
-                recv_sem=line_rsem.at[stage, OPPOSITE[side]],
-                device_id=target,
+                send_sem=line_ssem.at[stage, group, side],
+                recv_sem=line_rsem.at[stage, group, OPPOSITE[side]],
+                device_id=targets[side],
                 device_id_type=MESH,
             )
             copy.start()
             copies.append(copy)
         return copies
 
-    def put_corners(stage, corners):
-        for k in range(4):
-            corner_send[stage, k] = jnp.sum(corners[k], axis=0, keepdims=True)
-
-    def complete(q, stage):
-        borders = [corner_recv[stage, k] for k in range(4)]
-        return add_borders(load(rate, q), q, line_recv.at[stage], borders)
+    def extra_of(q, stage, group):
+        rows = [corner_recv[stage, group, k] for k in range(4)]
+        return borders_of(q - 4 * group, line_recv.at[stage, group], rows)
 
     no_corners = tuple(jnp.zeros((8, HALF), jnp.float32) for _ in range(4))
-
-    corners = lax.fori_loop(
-        0, 6, lambda q, c: tend(q, load(state, q), 0, c, False), no_corners, unroll=True
-    )
-    corners = tend(6, load(state, 6), 0, corners, True)
-    put_corners(0, corners)
-    pl.semaphore_wait(barrier, len(targets) + len(peers))
-    sends = exchange(0)
-    for copy in sends:
-        copy.wait_recv()
-
-    v = complete(6, 0)
-    for half in range(2):
-        for n in range(NODES):
-            shared[pl.ds(n, 1), pl.ds(HALF * half, HALF)] = v[half][n][4:5, :]
-    scale[...] = time_step / shared[...]
-
-    def advance(q, v, corners, mixed):
-        h = load(state, q)
-        for half in range(2):
-            c = scaled(half)
-            for n in range(NODES):
-                middle = h[half][n] + c[n] * v[half][n]
-                state[q, n, :, pl.ds(HALF * half, HALF)] = h[half][n] + middle
-                h[half][n] = middle
-        return tend(q, h, 1, corners, mixed)
-
-    corners = advance(6, v, no_corners, True)
-    corners = lax.fori_loop(
-        0, 6, lambda q, c: advance(q, complete(q, 0), c, False), corners, unroll=True
-    )
-    put_corners(1, corners)
-    second_sends = exchange(1)
-    for copy in second_sends:
-        copy.wait_recv()
-
-    def finish(q):
-        v = complete(q, 1)
-        h = load(state, q)
-        for half in range(2):
-            c = scaled(half)
-            for n in range(NODES):
-                h[half][n] = 0.5 * (h[half][n] + c[n] * v[half][n])
-        return h
-
-    h = finish(6)
-    for half in range(2):
-        at = pl.ds(HALF * half, HALF)
-        for n in range(NODES):
-            for l in range(2):
-                last[l, pl.ds(n, 1), at] = h[half][n][2 * l : 2 * l + 1, :]
-                thick[l, pl.ds(n, 1), at] = h[half][n][2 * l + 1 : 2 * l + 2, :]
-    column[...] = thick[0] + thick[1]
-    column_copies = []
-    for k, peer in enumerate(peers):
-        copy = pltpu.make_async_remote_copy(
-            src_ref=column,
-            dst_ref=columns.at[k],
-            send_sem=column_ssem.at[k],
-            recv_sem=column_rsem.at[k],
-            device_id=peer,
-            device_id_type=MESH,
-        )
-        copy.start()
-        column_copies.append(copy)
+    tiles_of = ((1, 4), (4, 7))
+
+    def first(q, corners, group, mixed=False):
+        v = rates_of(q, load(state, q), mixed)
+        save(rate, q, v)
+        return pack(v, q, 0, group, corners)
+
+    first_sends, second_sends = [], []
+    for group in range(2):
+        corners = first(0, no_corners, 0, True) if group == 0 else no_corners
+        corners = lax.fori_loop(
+            *tiles_of[group], lambda q, c: first(q, c, group), corners, unroll=True
+        )
+        if group == 0:
+            pl.semaphore_wait(barrier, len(targets) + len(peers))
+        first_sends.append(exchange(0, group, corners))
 
     below = {"lev": lax.rem(level + n_lev - 1, n_lev)}
     above = {"lev": lax.rem(level + 1, n_lev)}
+    has_below, has_above = level > 0, level < n_lev - 1
 
     def ratio_copy(t, l):
         return pltpu.make_async_remote_copy(
@@ -489,31 +460,134 @@
             device_id_type=MESH,
         )
 
-    has_below, has_above = level > 0, level < n_lev - 1
-
     def send_ratios(t):
         pl.when(has_below)(lambda: ratio_copy(t, 0).start())
         pl.when(has_above)(lambda: ratio_copy(t, 1).start())
 
-    for l in range(2):
-        inverse[l] = 1.0 / thick[l]
-        last_ratio[l] = last[l] * inverse[l]
-    send_ratios(3)
-
-    for t in range(3):
-
-        def edge(l, carry, t=t):
-            q = 2 * t + l
-            h = finish(q)
+    def edge_copy(l):
+        return pltpu.make_async_remote_copy(
+            src_ref=edge_send.at[l],
+            dst_ref=edge_recv.at[l],
+            send_sem=edge_ssem.at[l],
+            recv_sem=edge_rsem.at[l],
+            device_id=below if l == 0 else above,
+            device_id_type=MESH,
+        )
+
+    def second(q, corners, group, mixed=False):
+        v = load(rate, q)
+        extra = extra_of(q, 0, group)
+        for half in range(2):
+            for n in extra[half]:
+                v[half][n] = v[half][n] + extra[half][n]
+        if mixed:
+            for half in range(2):
+                for n in range(NODES):
+                    shared[pl.ds(n, 1), pl.ds(HALF * half, HALF)] = v[half][n][4:5, :]
+            scale[...] = time_step / shared[...]
+        h = load(state, q)
+        for half in range(2):
+            c = scaled(half)
+            for n in range(NODES):
+                middle = h[half][n] + c[n] * v[half][n]
+                state[q, n, :, pl.ds(HALF * half, HALF)] = h[half][n] + middle
+                h[half][n] = middle
+        v = rates_of(q, h, mixed)
+        h = load(state, q)
+        for half in range(2):
+            c = scaled(half)
+            for n in range(NODES):
+                h[half][n] = 0.5 * (h[half][n] + c[n] * v[half][n])
+        save(state, q, h)
+        if mixed:
+            split_mixed(h)
+            for l in range(2):
+                last_ratio[l] = last[l] * inverse[l]
+        else:
+            t, l = (q - 1) // 2, (q - 1) % 2
             for half in range(2):
                 at = pl.ds(HALF * half, HALF)
                 for n in range(NODES):
-                    state[q, n, :, at] = h[half][n]
                     ratio[t, l, n, :, at] = h[half][n] * inverse[l, pl.ds(n, 1), at]
-            return carry
-
-        lax.fori_loop(0, 2, edge, 0, unroll=True)
-        send_ratios(t)
+        return pack(v, q, 1, group, corners)
+
+    def split_mixed(h):
+        for half in range(2):
+            at = pl.ds(HALF * half, HALF)
+            for n in range(NODES):
+                for l in range(2):
+                    last[l, pl.ds(n, 1), at] = h[half][n][2 * l : 2 * l + 1, :]
+                    thick[l, pl.ds(n, 1), at] = h[half][n][2 * l + 1 : 2 * l + 2, :]
+        for l in range(2):
+            inverse[l] = 1.0 / thick[l]
+
+    for group in range(2):
+        for copy in first_sends[group]:
+            copy.wait_recv()
+        corners = second(0, no_corners, 0, True) if group == 0 else no_corners
+        corners = lax.fori_loop(
+            *tiles_of[group], lambda q, c: second(q, c, group), corners, unroll=True
+        )
+        second_sends.append(exchange(1, group, corners))
+        for t in ((3, 0), (1, 2))[group]:
+            send_ratios(t)
+
+    def finish(q, group, mixed=False):
+        extra = extra_of(q, 1, group)
+        h = load(state, q)
+        for half in range(2):
+            c = scaled(half)
+            at = pl.ds(HALF * half, HALF)
+            for n in extra[half]:
+                h[half][n] = h[half][n] + 0.5 * (c[n] * extra[half][n])
+                state[q, n, :, at] = h[half][n]
+        return h
+
+    def send_outline(q, h, l, slot, factor):
+        r = [[h[half][n] * factor(half, n) for n in range(NODES)] for half in range(2)]
+        for side, half, value in lines_of(r, slot):
+            edge_send[l, side, half] += value
+
+    def finish_levels(q, carry, group):
+        t, l = (q - 1) // 2, (q - 1) % 2
+        h = finish(q, group)
+        send_outline(
+            q, h, l, t, lambda half, n: inverse[l, pl.ds(n, 1), pl.ds(HALF * half, HALF)]
+        )
+        return carry
+
+    column_copies = []
+    for group in range(2):
+        for copy in second_sends[group]:
+            copy.wait_recv()
+        if group == 0:
+            h = finish(0, 0)
+            split_mixed(h)
+            column[...] = thick[0] + thick[1]
+            for k, peer in enumerate(peers):
+                copy = pltpu.make_async_remote_copy(
+                    src_ref=column,
+                    dst_ref=columns.at[k],
+                    send_sem=column_ssem.at[k],
+                    recv_sem=column_rsem.at[k],
+                    device_id=peer,
+                    device_id_type=MESH,
+                )
+                copy.start()
+                column_copies.append(copy)
+            for l in range(2):
+                send_outline(
+                    0,
+                    h,
+                    l,
+                    3,
+                    lambda half, n: inverse[l, pl.ds(n, 1), pl.ds(HALF * half, HALF)],
+                )
+        lax.fori_loop(
+            *tiles_of[group], lambda q, c: finish_levels(q, c, group), 0, unroll=True
+        )
+    pl.when(has_below)(lambda: edge_copy(0).start())
+    pl.when(has_above)(lambda: edge_copy(1).start())
 
     for copy in column_copies:
         copy.wait_recv()
@@ -552,10 +626,22 @@
         high = d[2] * jnp.where(d[2] > 0.0, own_ratio[1], ratio_above)
         return (carried[0] + low - middle) * d[3], (carried[1] + middle - high) * d[4]
 
+    pl.when(has_above)(lambda: edge_copy(0).wait_recv())
+    pl.when(has_below)(lambda: edge_copy(1).wait_recv())
     wait_ratios(3)
+    for l in range(2):
+        for half, n, mask, value in placed_lines(3, edge_recv.at[l]):
+            row, at = pl.ds(n, 1), pl.ds(HALF * half, HALF)
+            last_recv[l, row, at] = jnp.where(
+                mask[0:1], value[2 * l : 2 * l + 1], last_recv[l, row, at]
+            )
     d = [delta[k] for k in range(5)]
     first, second = remapped(
-        d, [last[0], last[1]], [last_ratio[0], last_ratio[1]], last_recv[0], last_recv[1]
+        d,
+        [last[0], last[1]],
+        [last[0] * inverse[0], last[1] * inverse[1]],
+        last_recv[0],
+        last_recv[1],
     )
     rows = permuted(jnp.concatenate([first, second, surface_rows], axis=0), tables[1])
     last_rows[...] = rows
@@ -570,17 +656,25 @@
 
     for t in range(3):
         wait_ratios(t)
+        beside_block = []
+        for l in range(2):
+            r = load(ratio_recv.at[t], l)
+            for half, n, mask, value in placed_lines(t, edge_recv.at[l]):
+                r[half][n] = jnp.where(mask, value, r[half][n])
+            beside_block.append(r)
         pairs = []
         for n in range(NODES):
-            d = [delta[k, pl.ds(n, 1), :] for k in range(5)]
+            parts = []
+            for half in range(2):
+                at = pl.ds(HALF * half, HALF)
+                d = [delta[k, pl.ds(n, 1), at] for k in range(5)]
+                carried = [state[2 * t + 1 + l, n, :, at] for l in range(2)]
+                own_ratio = [carried[l] * inverse[l, pl.ds(n, 1), at] for l in range(2)]
+                parts.append(
+                    remapped(d, carried, own_ratio, beside_block[0][half][n], beside_block[1][half][n])
+                )
             pairs.append(
-                remapped(
-                    d,
-                    [state[2 * t, n], state[2 * t + 1, n]],
-                    [ratio[t, 0, n], ratio[t, 1, n]],
-                    ratio_recv[t, 0, n],
-                    ratio_recv[t, 1, n],
-                )
+                [jnp.concatenate([parts[0][l], parts[1][l]], axis=1) for l in range(2)]
             )
         for l in range(2):
             tiles = permuted(jnp.concatenate([pair[l] for pair in pairs], axis=0), tables[1])
@@ -601,11 +695,13 @@
 
     for copy in out_copies:
         copy.wait()
-    for copy in sends + second_sends + column_copies:
+    for copy in sum(first_sends + second_sends, column_copies):
         copy.wait_send()
     for t in range(4):
         pl.when(has_below)(lambda t=t: ratio_copy(t, 0).wait_send())
         pl.when(has_above)(lambda t=t: ratio_copy(t, 1).wait_send())
+    pl.when(has_below)(lambda: edge_copy(0).wait_send())
+    pl.when(has_above)(lambda: edge_copy(1).wait_send())
 
 
 def per_device(n_elem, n_lev, tracers, layer_mass, winds, metric, neighbours):
@@ -627,10 +723,10 @@
         pltpu.VMEM((NODES, width), f32),
         pltpu.VMEM((NODES, width), f32),
         pltpu.VMEM((NODES, width), f32),
-        pltpu.VMEM((2, 4, 2, 2, 8, HALF), f32),
-        pltpu.VMEM((2, 4, 2, 2, 8, HALF), f32),
-        pltpu.VMEM((2, 4, 1, HALF), f32),
-        pltpu.VMEM((2, 4, 1, HALF), f32),
+        pltpu.VMEM((2, 2, 4, 2, 8, HALF), f32),
+        pltpu.VMEM((2, 2, 4, 2, 8, HALF), f32),
+        pltpu.VMEM((2, 2, 4, 1, HALF), f32),
+        pltpu.VMEM((2, 2, 4, 1, HALF), f32),
         pltpu.VMEM((2, NODES, width), f32),
         pltpu.VMEM((2, NODES, width), f32),
         pltpu.VMEM((2, NODES, width), f32),
@@ -640,18 +736,22 @@
         pltpu.VMEM((3, 2) + tile, f32),
         pltpu.VMEM((2, NODES, width), f32),
         pltpu.VMEM((2, NODES, width), f32),
+        pltpu.VMEM((2, 4, 2, 8, HALF), f32),
+        pltpu.VMEM((2, 4, 2, 8, HALF), f32),
         pltpu.VMEM((5, NODES, width), f32),
         pltpu.VMEM((2, 768, HALF), f32),
         pltpu.VMEM((3 * NODES, width), f32),
         dma((2,)),
         dma((5,)),
         dma((4, 2)),
-        dma((2, 8)),
-        dma((2, 8)),
+        dma((2, 2, 8)),
+        dma((2, 2, 8)),
         dma((n_lev - 1,)),
         dma((n_lev - 1,)),
         dma((4, 2)),
         dma((4, 2)),
+        dma((2,)),
+        dma((2,)),
     ]
     out, surface = pl.pallas_call(
         functools.partial(kernel, n_elem, n_lev),

time: 77.1 us -> 73.2 us (0.949)
  Pallas kernels: 73.6 us -> 69.4 us
    pallas_call x1, Pallas kernels: 73.6 us -> 69.4 us  [per_device(): pl.pallas_call(functools.partial(kernel, n_elem, n_lev), out_shape=(jax.S...]
where the time goes in v2:
time: 73.2 us; the launch traced here: 72.8 us
  Pallas kernels  69.4 us (95%)
  local copies, waits for them, and re-layouts  2.73 us (4%)
    pallas_call x1, Pallas kernels, per_device(): pl.pallas_call(functools.partial(kernel, n_elem, n_lev), out_shape=(jax.S...  69.4 us
    unnamed x4, local copies, waits for them, and re-layouts  2.73 us

profile of v2, /device:TPU:33, one launch (start us, length us, event | category | flops | bytes accessed | tf_op | source)
XLA Modules:
  0.0 72.8 jit_solution(11539639996942466438)
XLA Ops:
  0.6 69.4 %transport.1 = (f32[800,256]{1,0:T(8,128)}, f32[16,256]{1,0:T(8,128)}) custom-call(f32[800,256]{1,0:T(8,128)} %bitcast.5, f32[32,256]{1,0:T(8,128)} %bitcast.8, f32[64,256]{1,0:T(8,128)} %bitcast.7, f32[16,256]{1,0:T(8,128)} %metric.1, s32[8,256]{1,0:T(8,128)} %bitcast.9), custom_call_target="tpu_custom_call" | custom-call | tf_op jit(solution)/shard_map/transport/pallas_call | solution.py:756
  70.1 0.0 copy-start
  70.1 2.1 %copy.9 = f32[25,2,16,256]{3,2,1,0:T(8,128)} copy(f32[25,2,16,256]{3,2,1,0:T(8,128)} %bitcast.6) | data formatting | bytes 1638400
  72.2 0.0 copy-done
  72.2 0.6 copy.10
Async XLA Ops:
  70.1 2.1 %copy-start = (f32[16,256]{1,0:T(8,128)S(1)}, f32[16,256]{1,0:T(8,128)}, u32[]{:S(2)}) copy-start(f32[16,256]{1,0:T(8,128)} %get-tuple-element.9) | copy-start | bytes 49156

commit v3 on v2

--- a/solution.py
+++ b/solution.py
@@ -189,7 +189,7 @@
     metric,
     beside,
     out,
-    surf,
+    sums,
     near,
     raw,
     small_raw,
@@ -219,10 +219,8 @@
     edge_recv,
     delta,
     result,
-    last_rows,
     in_sem,
     small_sem,
-    out_sem,
     line_ssem,
     line_rsem,
     column_ssem,
@@ -592,13 +590,13 @@
     for copy in column_copies:
         copy.wait_recv()
     own_column = column[...]
-    total = own_column
+    others = jnp.zeros_like(own_column)
     under = jnp.zeros_like(own_column)
     for k in range(1, n_lev):
         part = columns[k - 1]
-        total = total + part
+        others = others + part
         under = under + jnp.where(k <= level, part, 0.0)
-    surface_rows = total
+    surface_rows = own_column + others
     levels = 2 * n_lev
 
     def as_float(k):
@@ -612,10 +610,6 @@
         if k > 0:
             under = under + thick[k - 1]
         delta[k] = under - surface_rows * fraction
-    for l in range(2):
-        share = (1.0 + 2.0 * as_float(2 * level + l) * (1.0 / (levels - 1))) * (0.5 / levels)
-        delta[3 + l] = 1.0 / (surface_rows * share)
-
     def wait_ratios(t):
         pl.when(has_above)(lambda: ratio_copy(t, 0).wait_recv())
         pl.when(has_below)(lambda: ratio_copy(t, 1).wait_recv())
@@ -624,7 +618,7 @@
         low = d[0] * jnp.where(d[0] > 0.0, ratio_below, own_ratio[0])
         middle = d[1] * jnp.where(d[1] > 0.0, own_ratio[0], own_ratio[1])
         high = d[2] * jnp.where(d[2] > 0.0, own_ratio[1], ratio_above)
-        return (carried[0] + low - middle) * d[3], (carried[1] + middle - high) * d[4]
+        return carried[0] + low - middle, carried[1] + middle - high
 
     pl.when(has_above)(lambda: edge_copy(0).wait_recv())
     pl.when(has_below)(lambda: edge_copy(1).wait_recv())
@@ -635,7 +629,7 @@
             last_recv[l, row, at] = jnp.where(
                 mask[0:1], value[2 * l : 2 * l + 1], last_recv[l, row, at]
             )
-    d = [delta[k] for k in range(5)]
+    d = [delta[k] for k in range(3)]
     first, second = remapped(
         d,
         [last[0], last[1]],
@@ -643,17 +637,16 @@
         last_recv[0],
         last_recv[1],
     )
-    rows = permuted(jnp.concatenate([first, second, surface_rows], axis=0), tables[1])
-    last_rows[...] = rows
-    out_copies = [
-        pltpu.make_async_copy(last_rows.at[pl.ds(32, 16)], surf, out_sem.at[3, 0]),
-        pltpu.make_async_copy(
-            last_rows.at[pl.ds(0, 32)], out.at[pl.ds(768, 32)], out_sem.at[3, 1]
-        ),
+    shares = [
+        surface_rows
+        * ((1.0 + 2.0 * as_float(2 * level + l) * (1.0 / (levels - 1))) * (0.5 / levels))
+        for l in range(2)
     ]
-    for copy in out_copies:
-        copy.start()
-
+    rows = permuted(
+        jnp.concatenate([first, second, own_column, others] + shares, axis=0), tables[1]
+    )
+    out[pl.ds(768, 32), :] = rows[0:32]
+    sums[...] = rows[32:96]
     for t in range(3):
         wait_ratios(t)
         beside_block = []
@@ -667,7 +660,7 @@
             parts = []
             for half in range(2):
                 at = pl.ds(HALF * half, HALF)
-                d = [delta[k, pl.ds(n, 1), at] for k in range(5)]
+                d = [delta[k, pl.ds(n, 1), at] for k in range(3)]
                 carried = [state[2 * t + 1 + l, n, :, at] for l in range(2)]
                 own_ratio = [carried[l] * inverse[l, pl.ds(n, 1), at] for l in range(2)]
                 parts.append(
@@ -685,16 +678,7 @@
                     ]
         rows = pl.ds(256 * t, 256)
         for half in range(2):
-            copy = pltpu.make_async_copy(
-                result.at[half, rows],
-                out.at[rows, pl.ds(HALF * half, HALF)],
-                out_sem.at[t, half],
-            )
-            copy.start()
-            out_copies.append(copy)
-
-    for copy in out_copies:
-        copy.wait()
+            out[rows, pl.ds(HALF * half, HALF)] = result[half, rows, :]
     for copy in sum(first_sends + second_sends, column_copies):
         copy.wait_send()
     for t in range(4):
@@ -707,7 +691,6 @@
 def per_device(n_elem, n_lev, tracers, layer_mass, winds, metric, neighbours):
     width = metric.shape[-1]
     f32 = jnp.float32
-    any_spec = pl.BlockSpec(memory_space=pl.ANY)
     tile = (NODES, 8, width)
     dma = pltpu.SemaphoreType.DMA
     scratch = [
@@ -738,12 +721,10 @@
         pltpu.VMEM((2, NODES, width), f32),
         pltpu.VMEM((2, 4, 2, 8, HALF), f32),
         pltpu.VMEM((2, 4, 2, 8, HALF), f32),
-        pltpu.VMEM((5, NODES, width), f32),
+        pltpu.VMEM((3, NODES, width), f32),
         pltpu.VMEM((2, 768, HALF), f32),
-        pltpu.VMEM((3 * NODES, width), f32),
         dma((2,)),
         dma((5,)),
-        dma((4, 2)),
         dma((2, 2, 8)),
         dma((2, 2, 8)),
         dma((n_lev - 1,)),
@@ -753,25 +734,37 @@
         dma((2,)),
         dma((2,)),
     ]
-    out, surface = pl.pallas_call(
+    result, sums = pl.pallas_call(
         functools.partial(kernel, n_elem, n_lev),
         out_shape=(
             jax.ShapeDtypeStruct((800, width), f32),
-            jax.ShapeDtypeStruct((NODES, width), f32),
+            jax.ShapeDtypeStruct((4 * NODES, width), f32),
         ),
-        in_specs=[any_spec] * 5,
-        out_specs=(any_spec, any_spec),
+        in_specs=[pl.BlockSpec(memory_space=pltpu.HBM)] * 5,
+        out_specs=(
+            pl.BlockSpec(memory_space=pltpu.VMEM),
+            pl.BlockSpec(memory_space=pltpu.VMEM),
+        ),
         scratch_shapes=scratch,
-        compiler_params=pltpu.CompilerParams(collective_id=0, has_side_effects=True),
+        compiler_params=pltpu.CompilerParams(
+            collective_id=0, has_side_effects=True, vmem_limit_bytes=24 * 1024 * 1024
+        ),
         name="transport",
     )(
-        tracers.reshape(-1, width),
-        layer_mass.reshape(-1, width),
-        winds.reshape(-1, width),
-        metric,
-        jnp.transpose(neighbours),
+        *[
+            pltpu.with_memory_space_constraint(x, pltpu.HBM)
+            for x in (
+                tracers.reshape(-1, width),
+                layer_mass.reshape(-1, width),
+                winds.reshape(-1, width),
+                metric,
+                jnp.transpose(neighbours),
+            )
+        ]
     )
-    return out.reshape(tracers.shape), surface
+    surface = sums[:NODES] + sums[NODES : 2 * NODES]
+    shares = sums[2 * NODES :].reshape(layer_mass.shape)
+    return result.reshape(tracers.shape) / shares, surface
 
 
 def solution(mesh):

time: 73.2 us -> 71.3 us (0.974)
  local copies, waits for them, and re-layouts: 2.73 us -> 0.01 us
  other arithmetic: 0 us -> 1.61 us
    unnamed x4 -> x0, local copies, waits for them, and re-layouts: 2.73 us -> none
    div x0 -> x1, other arithmetic: none -> 1 us  [per_device(): return (result.reshape(tracers.shape) / shares, surface)]
where the time goes in v3:
time: 71.3 us; the launch traced here: 71 us
  Pallas kernels  68.7 us (96%)
  other arithmetic  1.61 us (2%)
    pallas_call x1, Pallas kernels, per_device(): pl.pallas_call(functools.partial(kernel, n_elem, n_lev), out_shape=(jax.S...  68.7 us

profile of v3, /device:TPU:33, one launch (start us, length us, event | category | flops | bytes accessed | tf_op | source)
XLA Modules:
  0.0 71.0 jit_solution(3851478966099871340)
XLA Ops:
  0.6 68.7 %transport.1 = (f32[800,256]{1,0:T(8,128)S(1)}, f32[64,256]{1,0:T(8,128)S(1)}) custom-call(f32[800,256]{1,0:T(8,128)} %bitcast.7, f32[32,256]{1,0:T(8,128)} %bitcast.10, f32[64,256]{1,0:T(8,128)} %bitcast.9, f32[16,256]{1,0:T(8,128)} %metric.1, s32[8,256]{1,0:T(8,128)} %bitcast.11), custom_call_target="tpu_custom_call" | custom-call | tf_op jit(solution)/shard_map/transport/pallas_call | solution.py:737
  69.3 0.6 slice_add_fusion
  70.0 1.0 %broadcast_divide_fusion = f32[25,2,16,256]{3,2,1,0:T(8,128)} fusion(f32[25,2,16,256]{3,2,1,0:T(8,128)S(1)} %bitcast.6, f32[2,16,256]{2,1,0:T(8,128)S(1)} %bitcast.8), kind=kLoop, calls=%fused_computation | loop fusion | flops 204800 | bytes 1671168 | tf_op jit(solution)/shard_map/div | solution.py:767
  (1 shorter events, 0.0 us)

commit v4 on v3

--- a/solution.py
+++ b/solution.py
@@ -189,7 +189,7 @@
     metric,
     beside,
     out,
-    sums,
+    surface,
     near,
     raw,
     small_raw,
@@ -394,7 +394,7 @@
         return assembled_in_patch(v)
 
     def pack(v, q, stage, group, corners):
-        slot = q - 4 * group
+        slot = q - slot_base[group]
         for side, half, value in lines_of(v, slot):
             line_send[stage, group, side, half] += value
         return corners_of(v, slot, corners)
@@ -424,10 +424,11 @@
 
     def extra_of(q, stage, group):
         rows = [corner_recv[stage, group, k] for k in range(4)]
-        return borders_of(q - 4 * group, line_recv.at[stage, group], rows)
+        return borders_of(q - slot_base[group], line_recv.at[stage, group], rows)
 
     no_corners = tuple(jnp.zeros((8, HALF), jnp.float32) for _ in range(4))
-    tiles_of = ((1, 4), (4, 7))
+    tiles_of = ((1, 3), (3, 7))
+    slot_base = (0, 3)
 
     def first(q, corners, group, mixed=False):
         v = rates_of(q, load(state, q), mixed)
@@ -523,12 +524,15 @@
         for copy in first_sends[group]:
             copy.wait_recv()
         corners = second(0, no_corners, 0, True) if group == 0 else no_corners
-        corners = lax.fori_loop(
-            *tiles_of[group], lambda q, c: second(q, c, group), corners, unroll=True
-        )
+        for t in ((0,), (1, 2))[group]:
+            corners = lax.fori_loop(
+                2 * t + 1, 2 * t + 3, lambda q, c: second(q, c, group), corners, unroll=True
+            )
+            if t == 0:
+                send_ratios(3)
+            if t < 2:
+                send_ratios(t)
         second_sends.append(exchange(1, group, corners))
-        for t in ((3, 0), (1, 2))[group]:
-            send_ratios(t)
 
     def finish(q, group, mixed=False):
         extra = extra_of(q, 1, group)
@@ -586,6 +590,7 @@
         )
     pl.when(has_below)(lambda: edge_copy(0).start())
     pl.when(has_above)(lambda: edge_copy(1).start())
+    send_ratios(2)
 
     for copy in column_copies:
         copy.wait_recv()
@@ -610,6 +615,10 @@
         if k > 0:
             under = under + thick[k - 1]
         delta[k] = under - surface_rows * fraction
+    for l in range(2):
+        share = (1.0 + 2.0 * as_float(2 * level + l) * (1.0 / (levels - 1))) * (0.5 / levels)
+        delta[3 + l] = 1.0 / (surface_rows * share)
+
     def wait_ratios(t):
         pl.when(has_above)(lambda: ratio_copy(t, 0).wait_recv())
         pl.when(has_below)(lambda: ratio_copy(t, 1).wait_recv())
@@ -618,7 +627,7 @@
         low = d[0] * jnp.where(d[0] > 0.0, ratio_below, own_ratio[0])
         middle = d[1] * jnp.where(d[1] > 0.0, own_ratio[0], own_ratio[1])
         high = d[2] * jnp.where(d[2] > 0.0, own_ratio[1], ratio_above)
-        return carried[0] + low - middle, carried[1] + middle - high
+        return (carried[0] + low - middle) * d[3], (carried[1] + middle - high) * d[4]
 
     pl.when(has_above)(lambda: edge_copy(0).wait_recv())
     pl.when(has_below)(lambda: edge_copy(1).wait_recv())
@@ -629,7 +638,7 @@
             last_recv[l, row, at] = jnp.where(
                 mask[0:1], value[2 * l : 2 * l + 1], last_recv[l, row, at]
             )
-    d = [delta[k] for k in range(3)]
+    d = [delta[k] for k in range(5)]
     first, second = remapped(
         d,
         [last[0], last[1]],
@@ -637,16 +646,9 @@
         last_recv[0],
         last_recv[1],
     )
-    shares = [
-        surface_rows
-        * ((1.0 + 2.0 * as_float(2 * level + l) * (1.0 / (levels - 1))) * (0.5 / levels))
-        for l in range(2)
-    ]
-    rows = permuted(
-        jnp.concatenate([first, second, own_column, others] + shares, axis=0), tables[1]
-    )
+    rows = permuted(jnp.concatenate([first, second, surface_rows], axis=0), tables[1])
     out[pl.ds(768, 32), :] = rows[0:32]
-    sums[...] = rows[32:96]
+    surface[...] = rows[32:48]
     for t in range(3):
         wait_ratios(t)
         beside_block = []
@@ -660,7 +662,7 @@
             parts = []
             for half in range(2):
                 at = pl.ds(HALF * half, HALF)
-                d = [delta[k, pl.ds(n, 1), at] for k in range(3)]
+                d = [delta[k, pl.ds(n, 1), at] for k in range(5)]
                 carried = [state[2 * t + 1 + l, n, :, at] for l in range(2)]
                 own_ratio = [carried[l] * inverse[l, pl.ds(n, 1), at] for l in range(2)]
                 parts.append(
@@ -686,6 +688,17 @@
         pl.when(has_above)(lambda t=t: ratio_copy(t, 1).wait_send())
     pl.when(has_below)(lambda: edge_copy(0).wait_send())
     pl.when(has_above)(lambda: edge_copy(1).wait_send())
+
+
+def store(result, surface, out, surf, sem):
+    copies = [pltpu.make_async_copy(surface, surf, sem.at[4])]
+    for k in range(4):
+        rows = pl.ds(200 * k, 200)
+        copies.append(pltpu.make_async_copy(result.at[rows], out.at[rows], sem.at[k]))
+    for copy in copies:
+        copy.start()
+    for copy in copies:
+        copy.wait()
 
 
 def per_device(n_elem, n_lev, tracers, layer_mass, winds, metric, neighbours):
@@ -721,7 +734,7 @@
         pltpu.VMEM((2, NODES, width), f32),
         pltpu.VMEM((2, 4, 2, 8, HALF), f32),
         pltpu.VMEM((2, 4, 2, 8, HALF), f32),
-        pltpu.VMEM((3, NODES, width), f32),
+        pltpu.VMEM((5, NODES, width), f32),
         pltpu.VMEM((2, 768, HALF), f32),
         dma((2,)),
         dma((5,)),
@@ -734,17 +747,14 @@
         dma((2,)),
         dma((2,)),
     ]
-    result, sums = pl.pallas_call(
+    result, surface = pl.pallas_call(
         functools.partial(kernel, n_elem, n_lev),
         out_shape=(
             jax.ShapeDtypeStruct((800, width), f32),
-            jax.ShapeDtypeStruct((4 * NODES, width), f32),
+            jax.ShapeDtypeStruct((NODES, width), f32),
         ),
         in_specs=[pl.BlockSpec(memory_space=pltpu.HBM)] * 5,
-        out_specs=(
-            pl.BlockSpec(memory_space=pltpu.VMEM),
-            pl.BlockSpec(memory_space=pltpu.VMEM),
-        ),
+        out_specs=(pl.BlockSpec(memory_space=pltpu.VMEM),) * 2,
         scratch_shapes=scratch,
         compiler_params=pltpu.CompilerParams(
             collective_id=0, has_side_effects=True, vmem_limit_bytes=24 * 1024 * 1024
@@ -762,9 +772,19 @@
             )
         ]
     )
-    surface = sums[:NODES] + sums[NODES : 2 * NODES]
-    shares = sums[2 * NODES :].reshape(layer_mass.shape)
-    return result.reshape(tracers.shape) / shares, surface
+    result, surface = pl.pallas_call(
+        store,
+        out_shape=(
+            jax.ShapeDtypeStruct(result.shape, f32),
+            jax.ShapeDtypeStruct(surface.shape, f32),
+        ),
+        in_specs=[pl.BlockSpec(memory_space=pltpu.VMEM)] * 2,
+        out_specs=(pl.BlockSpec(memory_space=pltpu.HBM),) * 2,
+        scratch_shapes=[dma((5,))],
+        compiler_params=pltpu.CompilerParams(vmem_limit_bytes=24 * 1024 * 1024),
+        name="store",
+    )(result, surface)
+    return result.reshape(tracers.shape), surface
 
 
 def solution(mesh):

time: 71.3 us -> 68.4 us (0.959)
  other arithmetic: 1.61 us -> 0 us
  Pallas kernels: 68.7 us -> 67.6 us
    pallas_call x1, Pallas kernels: 68.7 us -> 66.6 us  [per_device(): pl.pallas_call(functools.partial(kernel, n_elem, n_lev), out_shape=(jax.S...]
    div x1 -> x0, other arithmetic: 1 us -> none  [per_device(): return (result.reshape(tracers.shape) / shares, surface)]
    pallas_call x0 -> x1, Pallas kernels: none -> 0.93 us  [per_device(): pl.pallas_call(store, out_shape=(jax.ShapeDtypeStruct(result.shape, f32),...]
where the time goes in v4:
time: 68.4 us; the launch traced here: 68.2 us
  Pallas kernels  67.6 us (99%)
    pallas_call x1, Pallas kernels, per_device(): pl.pallas_call(functools.partial(kernel, n_elem, n_lev), out_shape=(jax.S...  66.6 us

profile of v4, /device:TPU:33, one launch (start us, length us, event | category | flops | bytes accessed | tf_op | source)
XLA Modules:
  0.0 68.2 jit_solution(7244034274479400191)
XLA Ops:
  0.6 66.6 %transport.1 = (f32[800,256]{1,0:T(8,128)S(1)}, f32[16,256]{1,0:T(8,128)S(1)}) custom-call(f32[800,256]{1,0:T(8,128)} %bitcast.5, f32[32,256]{1,0:T(8,128)} %bitcast.7, f32[64,256]{1,0:T(8,128)} %bitcast.6, f32[16,256]{1,0:T(8,128)} %metric.1, s32[8,256]{1,0:T(8,128)} %bitcast.8), custom_call_target="tpu_custom_call" | custom-call | tf_op jit(solution)/shard_map/transport/pallas_call | solution.py:750
  67.3 0.9 %store.1 = (f32[800,256]{1,0:T(8,128)}, f32[16,256]{1,0:T(8,128)}) custom-call(f32[800,256]{1,0:T(8,128)S(1)} %get-tuple-element.6.result, f32[16,256]{1,0:T(8,128)S(1)} %get-tuple-element.7.surface), custom_call_target="tpu_custom_call" | custom-call | tf_op jit(solution)/shard_map/store/pallas_call | solution.py:775

commit v5 on v4

--- a/solution.py
+++ b/solution.py
@@ -172,8 +172,10 @@
     rest = x - high.astype(jnp.float32)
     middle = rest.astype(jnp.bfloat16)
     low = (rest - middle.astype(jnp.float32)).astype(jnp.bfloat16)
-    dot = functools.partial(jnp.dot, preferred_element_type=jnp.float32)
-    return dot(high, table) + dot(middle, table) + dot(low, table)
+    size = x.shape[0]
+    parts = jnp.concatenate([high, middle, low], axis=0)
+    y = jnp.dot(parts, table, preferred_element_type=jnp.float32)
+    return y[:size] + y[size : 2 * size] + y[2 * size :]
 
 
 def halves(x):
@@ -188,8 +190,8 @@
     winds,
     metric,
     beside,
-    out,
-    surface,
+    result,
+    last_rows,
     near,
     raw,
     small_raw,
@@ -218,7 +220,6 @@
     edge_send,
     edge_recv,
     delta,
-    result,
     in_sem,
     small_sem,
     line_ssem,
@@ -246,7 +247,7 @@
     peers = [{"lev": lax.rem(level + k, n_lev)} for k in range(1, n_lev)]
 
     barrier = pltpu.get_barrier_semaphore()
-    for target in targets + peers:
+    for target in targets[2:] + peers + targets[:2]:
         pl.semaphore_signal(barrier, inc=1, device_id=target, device_id_type=MESH)
 
     near_copy = pltpu.make_async_copy(beside, near, small_sem.at[0])
@@ -450,9 +451,16 @@
     has_below, has_above = level > 0, level < n_lev - 1
 
     def ratio_copy(t, l):
+        if t == 3:
+            source, landing = last_ratio.at[l], last_recv.at[l]
+        elif t < 2:
+            source, landing = ratio.at[t, l], ratio_recv.at[t, l]
+        else:
+            nodes = pl.ds(0, 4) if t == 2 else pl.ds(4, NODES - 4)
+            source, landing = ratio.at[2, l, nodes], ratio_recv.at[2, l, nodes]
         return pltpu.make_async_remote_copy(
-            src_ref=last_ratio.at[l] if t == 3 else ratio.at[t, l],
-            dst_ref=last_recv.at[l] if t == 3 else ratio_recv.at[t, l],
+            src_ref=source,
+            dst_ref=landing,
             send_sem=ratio_ssem.at[t, l],
             recv_sem=ratio_rsem.at[t, l],
             device_id=below if l == 0 else above,
@@ -577,6 +585,7 @@
                 )
                 copy.start()
                 column_copies.append(copy)
+            send_ratios(2)
             for l in range(2):
                 send_outline(
                     0,
@@ -590,7 +599,38 @@
         )
     pl.when(has_below)(lambda: edge_copy(0).start())
     pl.when(has_above)(lambda: edge_copy(1).start())
-    send_ratios(2)
+    send_ratios(4)
+
+    def wait_ratios(t):
+        pl.when(has_above)(lambda: ratio_copy(t, 0).wait_recv())
+        pl.when(has_below)(lambda: ratio_copy(t, 1).wait_recv())
+
+    def merge_outlines(t):
+        wait_ratios(t)
+        if t == 2:
+            wait_ratios(4)
+        for l in range(2):
+            found = {}
+            for half, n, mask, value in placed_lines(t, edge_recv.at[l]):
+                at = pl.ds(HALF * half, HALF)
+                before = found.get((half, n))
+                if before is None:
+                    before = ratio_recv[t, l, n, :, at]
+                found[half, n] = jnp.where(mask, value, before)
+            for (half, n), value in found.items():
+                ratio_recv[t, l, n, :, pl.ds(HALF * half, HALF)] = value
+
+    pl.when(has_above)(lambda: edge_copy(0).wait_recv())
+    pl.when(has_below)(lambda: edge_copy(1).wait_recv())
+    wait_ratios(3)
+    for l in range(2):
+        for half, n, mask, value in placed_lines(3, edge_recv.at[l]):
+            row, at = pl.ds(n, 1), pl.ds(HALF * half, HALF)
+            last_recv[l, row, at] = jnp.where(
+                mask[0:1], value[2 * l : 2 * l + 1], last_recv[l, row, at]
+            )
+    merge_outlines(0)
+    merge_outlines(1)
 
     for copy in column_copies:
         copy.wait_recv()
@@ -619,25 +659,12 @@
         share = (1.0 + 2.0 * as_float(2 * level + l) * (1.0 / (levels - 1))) * (0.5 / levels)
         delta[3 + l] = 1.0 / (surface_rows * share)
 
-    def wait_ratios(t):
-        pl.when(has_above)(lambda: ratio_copy(t, 0).wait_recv())
-        pl.when(has_below)(lambda: ratio_copy(t, 1).wait_recv())
-
     def remapped(d, carried, own_ratio, ratio_above, ratio_below):
         low = d[0] * jnp.where(d[0] > 0.0, ratio_below, own_ratio[0])
         middle = d[1] * jnp.where(d[1] > 0.0, own_ratio[0], own_ratio[1])
         high = d[2] * jnp.where(d[2] > 0.0, own_ratio[1], ratio_above)
         return (carried[0] + low - middle) * d[3], (carried[1] + middle - high) * d[4]
 
-    pl.when(has_above)(lambda: edge_copy(0).wait_recv())
-    pl.when(has_below)(lambda: edge_copy(1).wait_recv())
-    wait_ratios(3)
-    for l in range(2):
-        for half, n, mask, value in placed_lines(3, edge_recv.at[l]):
-            row, at = pl.ds(n, 1), pl.ds(HALF * half, HALF)
-            last_recv[l, row, at] = jnp.where(
-                mask[0:1], value[2 * l : 2 * l + 1], last_recv[l, row, at]
-            )
     d = [delta[k] for k in range(5)]
     first, second = remapped(
         d,
@@ -647,16 +674,10 @@
         last_recv[1],
     )
     rows = permuted(jnp.concatenate([first, second, surface_rows], axis=0), tables[1])
-    out[pl.ds(768, 32), :] = rows[0:32]
-    surface[...] = rows[32:48]
+    last_rows[...] = rows
     for t in range(3):
-        wait_ratios(t)
-        beside_block = []
-        for l in range(2):
-            r = load(ratio_recv.at[t], l)
-            for half, n, mask, value in placed_lines(t, edge_recv.at[l]):
-                r[half][n] = jnp.where(mask, value, r[half][n])
-            beside_block.append(r)
+        if t == 2:
+            merge_outlines(2)
         pairs = []
         for n in range(NODES):
             parts = []
@@ -666,35 +687,42 @@
                 carried = [state[2 * t + 1 + l, n, :, at] for l in range(2)]
                 own_ratio = [carried[l] * inverse[l, pl.ds(n, 1), at] for l in range(2)]
                 parts.append(
-                    remapped(d, carried, own_ratio, beside_block[0][half][n], beside_block[1][half][n])
+                    remapped(d, carried, own_ratio, ratio_recv[t, 0, n, :, at], ratio_recv[t, 1, n, :, at])
                 )
             pairs.append(
                 [jnp.concatenate([parts[0][l], parts[1][l]], axis=1) for l in range(2)]
             )
-        for l in range(2):
-            tiles = permuted(jnp.concatenate([pair[l] for pair in pairs], axis=0), tables[1])
-            for n in range(NODES):
-                for half in range(2):
-                    result[half, pl.ds(256 * t + 16 * l + n, 8, stride=32), :] = tiles[
-                        8 * n : 8 * n + 8, HALF * half : HALF * half + HALF
-                    ]
-        rows = pl.ds(256 * t, 256)
-        for half in range(2):
-            out[rows, pl.ds(HALF * half, HALF)] = result[half, rows, :]
+        tiles = permuted(
+            jnp.concatenate([pair[l] for l in range(2) for pair in pairs], axis=0), tables[1]
+        )
+        for k in range(2 * NODES):
+            for half in range(2):
+                result[half, pl.ds(256 * t + k, 8, stride=32), :] = tiles[
+                    8 * k : 8 * k + 8, HALF * half : HALF * half + HALF
+                ]
     for copy in sum(first_sends + second_sends, column_copies):
         copy.wait_send()
-    for t in range(4):
+    for t in range(5):
         pl.when(has_below)(lambda t=t: ratio_copy(t, 0).wait_send())
         pl.when(has_above)(lambda t=t: ratio_copy(t, 1).wait_send())
     pl.when(has_below)(lambda: edge_copy(0).wait_send())
     pl.when(has_above)(lambda: edge_copy(1).wait_send())
 
 
-def store(result, surface, out, surf, sem):
-    copies = [pltpu.make_async_copy(surface, surf, sem.at[4])]
-    for k in range(4):
-        rows = pl.ds(200 * k, 200)
-        copies.append(pltpu.make_async_copy(result.at[rows], out.at[rows], sem.at[k]))
+def store(result, last_rows, out, surf, sem):
+    copies = [
+        pltpu.make_async_copy(last_rows.at[pl.ds(32, 16)], surf, sem.at[0]),
+        pltpu.make_async_copy(last_rows.at[pl.ds(0, 32)], out.at[pl.ds(768, 32)], sem.at[1]),
+    ]
+    for half in range(2):
+        at = pl.ds(HALF * half, HALF)
+        for k in range(2):
+            rows = pl.ds(384 * k, 384)
+            copies.append(
+                pltpu.make_async_copy(
+                    result.at[half, rows], out.at[rows, at], sem.at[2 + 2 * half + k]
+                )
+            )
     for copy in copies:
         copy.start()
     for copy in copies:
@@ -735,23 +763,22 @@
         pltpu.VMEM((2, 4, 2, 8, HALF), f32),
         pltpu.VMEM((2, 4, 2, 8, HALF), f32),
         pltpu.VMEM((5, NODES, width), f32),
-        pltpu.VMEM((2, 768, HALF), f32),
         dma((2,)),
         dma((5,)),
         dma((2, 2, 8)),
         dma((2, 2, 8)),
         dma((n_lev - 1,)),
         dma((n_lev - 1,)),
-        dma((4, 2)),
-        dma((4, 2)),
+        dma((5, 2)),
+        dma((5, 2)),
         dma((2,)),
         dma((2,)),
     ]
-    result, surface = pl.pallas_call(
+    result, last_rows = pl.pallas_call(
         functools.partial(kernel, n_elem, n_lev),
         out_shape=(
-            jax.ShapeDtypeStruct((800, width), f32),
-            jax.ShapeDtypeStruct((NODES, width), f32),
+            jax.ShapeDtypeStruct((2, 768, HALF), f32),
+            jax.ShapeDtypeStruct((3 * NODES, width), f32),
         ),
         in_specs=[pl.BlockSpec(memory_space=pltpu.HBM)] * 5,
         out_specs=(pl.BlockSpec(memory_space=pltpu.VMEM),) * 2,
@@ -772,19 +799,19 @@
             )
         ]
     )
-    result, surface = pl.pallas_call(
+    out, surface = pl.pallas_call(
         store,
         out_shape=(
-            jax.ShapeDtypeStruct(result.shape, f32),
-            jax.ShapeDtypeStruct(surface.shape, f32),
+            jax.ShapeDtypeStruct((800, width), f32),
+            jax.ShapeDtypeStruct((NODES, width), f32),
         ),
         in_specs=[pl.BlockSpec(memory_space=pltpu.VMEM)] * 2,
         out_specs=(pl.BlockSpec(memory_space=pltpu.HBM),) * 2,
-        scratch_shapes=[dma((5,))],
+        scratch_shapes=[dma((6,))],
         compiler_params=pltpu.CompilerParams(vmem_limit_bytes=24 * 1024 * 1024),
         name="store",
-    )(result, surface)
-    return result.reshape(tracers.shape), surface
+    )(result, last_rows)
+    return out.reshape(tracers.shape), surface
 
 
 def solution(mesh):

time: 68.4 us -> 68.1 us (level)
  no operation moved by 1% of the time
where the time goes in v5:
time: 68.1 us; the launch traced here: 68 us
  Pallas kernels  67.3 us (99%)
    pallas_call x1, Pallas kernels, per_device(): pl.pallas_call(functools.partial(kernel, n_elem, n_lev), out_shape=(jax.S...  66.4 us

profile of v5, /device:TPU:33, one launch (start us, length us, event | category | flops | bytes accessed | tf_op | source)
XLA Modules:
  0.0 68.0 jit_solution(10196176945732043882)
XLA Ops:
  0.6 66.4 %transport.1 = (f32[2,768,128]{2,1,0:T(8,128)S(1)}, f32[48,256]{1,0:T(8,128)S(1)}) custom-call(f32[800,256]{1,0:T(8,128)} %bitcast.5, f32[32,256]{1,0:T(8,128)} %bitcast.7, f32[64,256]{1,0:T(8,128)} %bitcast.6, f32[16,256]{1,0:T(8,128)} %metric.1, s32[8,256]{1,0:T(8,128)} %bitcast.8), custom_call_target="tpu_custom_call" | custom-call | tf_op jit(solution)/shard_map/transport/pallas_call | solution.py:777
  67.0 0.9 %store.1 = (f32[800,256]{1,0:T(8,128)}, f32[16,256]{1,0:T(8,128)}) custom-call(f32[2,768,128]{2,1,0:T(8,128)S(1)} %get-tuple-element.6.result, f32[48,256]{1,0:T(8,128)S(1)} %get-tuple-element.7.last_rows), custom_call_target="tpu_custom_call" | custom-call | tf_op jit(solution)/shard_map/store/pallas_call | solution.py:802

commit v6 on v5

--- a/solution.py
+++ b/solution.py
@@ -491,20 +491,21 @@
             for half in range(2):
                 for n in range(NODES):
                     shared[pl.ds(n, 1), pl.ds(HALF * half, HALF)] = v[half][n][4:5, :]
-            scale[...] = time_step / shared[...]
+            scale[...] = (0.5 * time_step) / shared[...]
         h = load(state, q)
         for half in range(2):
             c = scaled(half)
             for n in range(NODES):
-                middle = h[half][n] + c[n] * v[half][n]
-                state[q, n, :, pl.ds(HALF * half, HALF)] = h[half][n] + middle
-                h[half][n] = middle
+                step = c[n] * v[half][n]
+                mean = h[half][n] + step
+                state[q, n, :, pl.ds(HALF * half, HALF)] = mean
+                h[half][n] = mean + step
         v = rates_of(q, h, mixed)
         h = load(state, q)
         for half in range(2):
             c = scaled(half)
             for n in range(NODES):
-                h[half][n] = 0.5 * (h[half][n] + c[n] * v[half][n])
+                h[half][n] = h[half][n] + c[n] * v[half][n]
         save(state, q, h)
         if mixed:
             split_mixed(h)
@@ -532,12 +533,12 @@
         for copy in first_sends[group]:
             copy.wait_recv()
         corners = second(0, no_corners, 0, True) if group == 0 else no_corners
+        if group == 0:
+            send_ratios(3)
         for t in ((0,), (1, 2))[group]:
             corners = lax.fori_loop(
                 2 * t + 1, 2 * t + 3, lambda q, c: second(q, c, group), corners, unroll=True
             )
-            if t == 0:
-                send_ratios(3)
             if t < 2:
                 send_ratios(t)
         second_sends.append(exchange(1, group, corners))
@@ -549,7 +550,7 @@
             c = scaled(half)
             at = pl.ds(HALF * half, HALF)
             for n in extra[half]:
-                h[half][n] = h[half][n] + 0.5 * (c[n] * extra[half][n])
+                h[half][n] = h[half][n] + c[n] * extra[half][n]
                 state[q, n, :, at] = h[half][n]
         return h
 

time: 68.1 us -> 67.9 us (level)
  no operation moved by 1% of the time
where the time goes in v6:
time: 67.9 us; the launch traced here: 67.8 us
  Pallas kernels  67.2 us (99%)
    pallas_call x1, Pallas kernels, per_device(): pl.pallas_call(functools.partial(kernel, n_elem, n_lev), out_shape=(jax.S...  66.2 us

profile of v6, /device:TPU:33, one launch (start us, length us, event | category | flops | bytes accessed | tf_op | source)
XLA Modules:
  0.0 67.8 jit_solution(6867450495710844149)
XLA Ops:
  0.6 66.2 %transport.1 = (f32[2,768,128]{2,1,0:T(8,128)S(1)}, f32[48,256]{1,0:T(8,128)S(1)}) custom-call(f32[800,256]{1,0:T(8,128)} %bitcast.5, f32[32,256]{1,0:T(8,128)} %bitcast.7, f32[64,256]{1,0:T(8,128)} %bitcast.6, f32[16,256]{1,0:T(8,128)} %metric.1, s32[8,256]{1,0:T(8,128)} %bitcast.8), custom_call_target="tpu_custom_call" | custom-call | tf_op jit(solution)/shard_map/transport/pallas_call | solution.py:778
  66.8 0.9 %store.1 = (f32[800,256]{1,0:T(8,128)}, f32[16,256]{1,0:T(8,128)}) custom-call(f32[2,768,128]{2,1,0:T(8,128)S(1)} %get-tuple-element.6.result, f32[48,256]{1,0:T(8,128)S(1)} %get-tuple-element.7.last_rows), custom_call_target="tpu_custom_call" | custom-call | tf_op jit(solution)/shard_map/store/pallas_call | solution.py:803

commit v7 on v6

--- a/solution.py
+++ b/solution.py
@@ -501,6 +501,13 @@
                 state[q, n, :, pl.ds(HALF * half, HALF)] = mean
                 h[half][n] = mean + step
         v = rates_of(q, h, mixed)
+        if group == 1:
+            save(rate, q, v)
+        else:
+            settle(q, v, mixed)
+        return pack(v, q, 1, group, corners)
+
+    def settle(q, v, mixed=False):
         h = load(state, q)
         for half in range(2):
             c = scaled(half)
@@ -517,7 +524,6 @@
                 at = pl.ds(HALF * half, HALF)
                 for n in range(NODES):
                     ratio[t, l, n, :, at] = h[half][n] * inverse[l, pl.ds(n, 1), at]
-        return pack(v, q, 1, group, corners)
 
     def split_mixed(h):
         for half in range(2):
@@ -535,13 +541,20 @@
         corners = second(0, no_corners, 0, True) if group == 0 else no_corners
         if group == 0:
             send_ratios(3)
-        for t in ((0,), (1, 2))[group]:
-            corners = lax.fori_loop(
-                2 * t + 1, 2 * t + 3, lambda q, c: second(q, c, group), corners, unroll=True
-            )
-            if t < 2:
-                send_ratios(t)
+        corners = lax.fori_loop(
+            *tiles_of[group], lambda q, c: second(q, c, group), corners, unroll=True
+        )
+        if group == 0:
+            send_ratios(0)
         second_sends.append(exchange(1, group, corners))
+
+    def settle_step(q, carry):
+        settle(q, load(rate, q))
+        return carry
+
+    lax.fori_loop(3, 5, settle_step, 0, unroll=True)
+    send_ratios(1)
+    lax.fori_loop(5, 7, settle_step, 0, unroll=True)
 
     def finish(q, group, mixed=False):
         extra = extra_of(q, 1, group)

time: 67.9 us -> 67.9 us (level)
  no operation moved by 1% of the time
where the time goes in v7:
time: 67.9 us; the launch traced here: 67.8 us
  Pallas kernels  67.1 us (99%)
    pallas_call x1, Pallas kernels, per_device(): pl.pallas_call(functools.partial(kernel, n_elem, n_lev), out_shape=(jax.S...  66.2 us

profile of v7, /device:TPU:33, one launch (start us, length us, event | category | flops | bytes accessed | tf_op | source)
XLA Modules:
  0.0 67.8 jit_solution(16417040849640303646)
XLA Ops:
  0.6 66.2 %transport.1 = (f32[2,768,128]{2,1,0:T(8,128)S(1)}, f32[48,256]{1,0:T(8,128)S(1)}) custom-call(f32[800,256]{1,0:T(8,128)} %bitcast.5, f32[32,256]{1,0:T(8,128)} %bitcast.7, f32[64,256]{1,0:T(8,128)} %bitcast.6, f32[16,256]{1,0:T(8,128)} %metric.1, s32[8,256]{1,0:T(8,128)} %bitcast.8), custom_call_target="tpu_custom_call" | custom-call | tf_op jit(solution)/shard_map/transport/pallas_call | solution.py:791
  66.8 0.9 %store.1 = (f32[800,256]{1,0:T(8,128)}, f32[16,256]{1,0:T(8,128)}) custom-call(f32[2,768,128]{2,1,0:T(8,128)S(1)} %get-tuple-element.6.result, f32[48,256]{1,0:T(8,128)S(1)} %get-tuple-element.7.last_rows), custom_call_target="tpu_custom_call" | custom-call | tf_op jit(solution)/shard_map/store/pallas_call | solution.py:816
